TPU v7x, 32 devices: a whole 2x2x4 slice. The times are simulated.
32 devices in a mesh: gx: 4 (over y, core), gy: 4 (over z), gz: 2 (over x).
Axes of the slice: x: 2, y: 2, z: 4, core: 2. Of those that a mesh axis runs over, the one named last changes fastest.
Arguments:
- order_param: float32 [16, 64, 256], P('gx', 'gy', 'gz'), may hold values from -1 to 1
- density: float32 [16, 64, 256], P('gx', 'gy', 'gz'), may hold values from 0.7 to 1.3
- velocity: float32 [3, 16, 64, 256], P(None, 'gx', 'gy', 'gz'), may hold values from -0.3 to 0.3
Outputs:
- final_order: float32 [16, 64, 256], P('gx', 'gy', 'gz')
- populations: float32 [19, 16, 64, 256], P(None, 'gx', 'gy', 'gz')
All inputs are finite; a program needn't handle non-finite values.
Results may differ from a plain program's by a relative error of at most 0.0001.
Values sent between devices are 32-bit elements; how exact they have to be, the bound alone decides.
A program may use at most 64 MiB of HBM per device.

v0:
```python
import functools

import jax
import jax.numpy as jnp
from jax import lax
from jax.experimental import pallas as pl
from jax.experimental.pallas import tpu as pltpu
from jax.sharding import PartitionSpec as P

ITERS = 5
MESH = pl.DeviceIdType.MESH
DIRS = [
    (0, 0, 0),
    (1, 0, 0),
    (-1, 0, 0),
    (0, 1, 0),
    (0, -1, 0),
    (0, 0, 1),
    (0, 0, -1),
    (1, 1, 0),
    (-1, -1, 0),
    (1, -1, 0),
    (-1, 1, 0),
    (1, 0, 1),
    (-1, 0, -1),
    (1, 0, -1),
    (-1, 0, 1),
    (0, 1, 1),
    (0, -1, -1),
    (0, 1, -1),
    (0, -1, 1),
]
WEIGHTS = [1.0 / 3.0] + [1.0 / 18.0] * 6 + [1.0 / 36.0] * 12
quadratic = -0.1
quartic = 0.1
stiffness = 0.02
mobility = 0.5
relax_time = 0.8

SIGNS = (1, -1)
INDEX = {1: 0, -1: 1}
CROSS = [{s: [i for i in range(19) if DIRS[i][d] == s] for s in SIGNS} for d in range(3)]
EDGES = [(a, b) for a in SIGNS for b in SIGNS]
LANES = 8


def neighbours():
    out = []
    for d in range(3):
        for s in SIGNS:
            out.append(tuple(s if k == d else 0 for k in range(3)))
    out += [(a, b, 0) for a, b in EDGES]
    out += [(a, 0, b) for a, b in EDGES]
    out += [(0, a, b) for a, b in EDGES]
    return out


def kernel(sizes, order_in, dens_in, vel_in, order, pops, post, *scratch):
    (ax, ay, az, rax, ray, raz, ae, rae) = scratch[0:8]
    (by, bz, rbx, rby, rbz, be, rbe) = scratch[8:15]
    (cx_, cy_, cz_, rcx, rcy, rcz) = scratch[15:21]
    (sa, ra, sb, rb, sc, rc) = scratch[21:27]
    X, Y, Z = order.shape
    me = [lax.axis_index(a) for a in ("gx", "gy", "gz")]

    def device(off):
        return {
            a: lax.rem(me[k] + (off[k] + sizes[k]), sizes[k]) if off[k] else me[k]
            for k, a in enumerate(("gx", "gy", "gz"))
        }

    barrier = pltpu.get_barrier_semaphore()
    for off in neighbours():
        pl.semaphore_signal(barrier, inc=1, device_id=device(off), device_id_type=MESH)

    lane = lax.broadcasted_iota(jnp.int32, (Y, Z), 1)
    row = lax.broadcasted_iota(jnp.int32, (Y, Z), 0)
    lane8 = lax.broadcasted_iota(jnp.int32, (8, Z), 1)
    row8 = lax.broadcasted_iota(jnp.int32, (8, Z), 0)
    lane1 = lax.broadcasted_iota(jnp.int32, (1, Z), 1)

    def roll(v, s, axis):
        s = s % v.shape[axis]
        return v if s == 0 else pltpu.roll(v, s, axis)

    def zend(s):
        return 0 if s == 1 else Z - 1

    def yend(s):
        return 0 if s == 1 else Y - 1

    def zshift(v, s, packed, at):
        col = roll(packed, zend(s) - at, 1)
        return jnp.where(lane == zend(s), col, roll(v, s, 1))

    def yshift(v, s, halo):
        return jnp.where(row == yend(s), jnp.broadcast_to(halo, v.shape), roll(v, s, 0))

    def zinsert(v, s, col, lanes):
        return jnp.where(lanes == zend(s), jnp.broadcast_to(col, v.shape), roll(v, s, 1))

    def to_row(v, z):
        col = jnp.broadcast_to(v[:, z : z + 1], v.shape)
        return jnp.sum(jnp.where(lane == row, col, 0.0), axis=0, keepdims=True)

    def to_col(v, lanes, rows):
        v = jnp.broadcast_to(v, lanes.shape)
        return jnp.sum(jnp.where(lanes == rows, v, 0.0), axis=1, keepdims=True)

    def xsrc(s):
        return X - 1 if s == 1 else 0

    def ysrc(s):
        return Y - 1 if s == 1 else 0

    def zsrc(s):
        return Z - 1 if s == 1 else 0

    def corners(planes, b, c):
        y, acc = ysrc(b), jnp.zeros((1, Z), jnp.float32)
        for x in range(X):
            cells = roll(planes[x][y : y + 1, :], 1 + x - zsrc(c), 1)
            acc = jnp.where(lane1 == 1 + x, cells, acc)
        return acc

    def pack(fields, s):
        acc = jnp.zeros((Y, Z), jnp.float32)
        for slot, planes in enumerate(fields):
            for x in range(X):
                at = slot * LANES + 1 + x
                depth_lane = planes[x][1]
                acc = jnp.where(lane == at, roll(planes[x][0], at - depth_lane, 1), acc)
        return acc

    def run(messages, ssem, rsem, first=0):
        copies = []
        messages = sorted(messages, key=lambda m: (m[2][1] == 0, -sum(map(abs, m[2]))))
        for k, (src, dst, off) in enumerate(messages, first):
            copy = pltpu.make_async_remote_copy(
                src_ref=src,
                dst_ref=dst,
                send_sem=ssem.at[k],
                recv_sem=rsem.at[k],
                device_id=device(off),
                device_id_type=MESH,
            )
            copy.start()
            copies.append(copy)
        return copies

    def finish(copies):
        for copy in copies:
            copy.wait_recv()
        for copy in copies:
            copy.wait_send()

    for ref in (ay, by, cy_):
        ref[...] = jnp.zeros_like(ref)

    for x in range(X):
        order[x] = order_in[x]
        r = dens_in[x]
        u = [vel_in[d, x] for d in range(3)]
        usq = 1.0 - 1.5 * (u[0] * u[0] + u[1] * u[1] + u[2] * u[2])
        for i in range(19):
            along = None
            for d in range(3):
                if DIRS[i][d]:
                    t = u[d] if DIRS[i][d] == 1 else -u[d]
                    along = t if along is None else along + t
            if along is None:
                pops[i, x] = WEIGHTS[i] * r * usq
            else:
                pops[i, x] = WEIGHTS[i] * r * (usq + 3.0 * along + 4.5 * along * along)
    pl.semaphore_wait(barrier, len(neighbours()))

    outer_first = sorted(range(X), key=lambda x: (min(x, X - 1 - x), x))

    def moments(ps):
        rho = ps[0]
        for i in range(1, 19):
            rho = rho + ps[i]
        moms = []
        for d in range(3):
            up = functools.reduce(lambda a, b: a + b, [ps[i] for i in CROSS[d][1]])
            down = functools.reduce(lambda a, b: a + b, [ps[i] for i in CROSS[d][-1]])
            moms.append(up - down)
        return rho, moms

    def chemical(o, beside):
        return quadratic * o + quartic * o * o * o - stiffness * (beside - 6.0 * o)

    def step(_, carry):
        O = [order[x] for x in range(X)]
        for s in SIGNS:
            si = INDEX[s]
            for depth in range(2):
                y = Y - 1 - depth if s == 1 else depth
                for x in range(X):
                    by[si, depth, 1 + x : 2 + x, :] = O[x][y : y + 1, :]
        messages = []
        for s in SIGNS:
            si = INDEX[s]
            planes = order.at[pl.ds(X - 2, 2)] if s == 1 else order.at[pl.ds(0, 2)]
            messages.append((planes, rbx.at[si], (s, 0, 0)))
            messages.append((by.at[si], rby.at[si], (0, s, 0)))
        for e, (a, b) in enumerate(EDGES):
            be[e] = O[xsrc(a)][ysrc(b) : ysrc(b) + 1, :]
            be[4 + e] = to_row(O[xsrc(a)], zsrc(b))
            be[8 + e] = corners(O, a, b)
            messages.append((be.at[e], rbe.at[e], (a, b, 0)))
            messages.append((be.at[4 + e], rbe.at[4 + e], (a, 0, b)))
            messages.append((be.at[8 + e], rbe.at[8 + e], (0, a, b)))
        flying = run(messages, sb, rb)
        messages = []
        for s in SIGNS:
            si = INDEX[s]
            bz[si] = pack(
                [
                    [(O[x], Z - 1 - depth if s == 1 else depth) for x in range(X)]
                    for depth in range(2)
                ],
                s,
            )
            messages.append((bz.at[si], rbz.at[si], (0, 0, s)))
        flying = flying + run(messages, sb, rb, len(flying))

        keep = 1.0 - 1.0 / relax_time
        mix = 1.0 / relax_time - 1.0

        def along(i, w):
            a = None
            for d in range(3):
                if DIRS[i][d]:
                    t = w[d] if DIRS[i][d] == 1 else -w[d]
                    a = t if a is None else a + t
            return a

        moved = []
        for x in range(X):
            ps = [pops[i, x] for i in range(19)]
            rho, moms = moments(ps)
            inv = 1.0 / rho
            u = [m * inv for m in moms]
            flat = (mix * rho) * (1.0 - 1.5 * (u[0] * u[0] + u[1] * u[1] + u[2] * u[2]))
            post[0, x] = keep * ps[0] + WEIGHTS[0] * flat
            for i in range(1, 19, 2):
                a = along(i, u)
                even = WEIGHTS[i] * flat + (4.5 * mix * WEIGHTS[i]) * rho * (a * a)
                odd = (3.0 * mix * WEIGHTS[i]) * rho * a
                post[i, x] = keep * ps[i] + even + odd
                post[i + 1, x] = keep * ps[i + 1] + even - odd
            moved.append((rho, inv, u))
        finish(flying)

        edge = {ab: e for e, ab in enumerate(EDGES)}
        OX = {-2: rbx[0, 0], -1: rbx[0, 1], X: rbx[1, 0], X + 1: rbx[1, 1]}
        for x in range(X):
            OX[x] = O[x]

        def order_y(x, s):
            return yshift(O[x], s, rby[INDEX[s], 0, 1 + x : 2 + x, :])

        def order_z(x, s):
            return zshift(O[x], s, rbz[INDEX[s]], 1 + x)

        C, pairs = {}, []
        for x in range(X):
            near = {(0, 1): OX[x - 1], (0, -1): OX[x + 1]}
            for s in SIGNS:
                near[(1, s)], near[(2, s)] = order_y(x, s), order_z(x, s)
            C[x] = chemical(O[x], functools.reduce(lambda a, b: a + b, near.values()))
            pairs.append({k: O[x] + v for k, v in near.items()})
        for s in SIGNS:
            x = -1 if s == 1 else X
            p = OX[x]
            beside = OX[x - 1] + OX[x + 1]
            for t in SIGNS:
                e = edge[(s, t)]
                beside = beside + yshift(p, t, rbe[e])
                beside = beside + zinsert(p, t, to_col(rbe[4 + e], lane, row), lane)
            C[x] = chemical(p, beside)
        CY, CZ = {}, {}
        for s in SIGNS:
            near = rby[INDEX[s], 0]
            full = jnp.where(row8 == 0, jnp.broadcast_to(rbe[edge[(1, s)]], near.shape), near)
            after = jnp.broadcast_to(rbe[edge[(-1, s)]], near.shape)
            full = jnp.where(row8 == X + 1, after, full)
            beside = rby[INDEX[s], 1] + by[INDEX[-s], 0] + roll(full, 1, 0) + roll(full, -1, 0)
            for t in SIGNS:
                col = to_col(rbe[8 + edge[(s, t)]], lane8, row8)
                beside = beside + zinsert(near, t, col, lane8)
            CY[s] = chemical(near, beside)

            near = rbz[INDEX[s]]
            before = jnp.broadcast_to(to_col(rbe[4 + edge[(1, s)]], lane, row), near.shape)
            after = jnp.broadcast_to(to_col(rbe[4 + edge[(-1, s)]], lane, row), near.shape)
            full = jnp.where(lane == 0, before, near)
            full = jnp.where(lane == X + 1, after, full)
            beside = roll(near, -LANES, 1) + bz[INDEX[-s]] + roll(full, 1, 1) + roll(full, -1, 1)
            for t in SIGNS:
                beside = beside + yshift(near, t, rbe[8 + edge[(t, s)]])
            CZ[s] = chemical(near, beside)

        diffused = {}
        flying = []
        for place, x in enumerate(outer_first):
            c = C[x]
            cy_up = yshift(c, -1, CY[-1][1 + x : 2 + x, :])
            cy_dn = yshift(c, 1, CY[1][1 + x : 2 + x, :])
            cz_up = zshift(c, -1, CZ[-1], 1 + x)
            cz_dn = zshift(c, 1, CZ[1], 1 + x)
            diffused[x] = C[x + 1] + C[x - 1] + cy_up + cy_dn + cz_up + cz_dn - 6.0 * c
            scale = -0.5 * O[x]
            force = [scale * (C[x + 1] - C[x - 1]), scale * (cy_up - cy_dn), scale * (cz_up - cz_dn)]
            rho, inv, u = moved[x]
            v = [u[d] + force[d] * inv for d in range(3)]
            flat = rho * (1.0 - 1.5 * (v[0] * v[0] + v[1] * v[1] + v[2] * v[2]))
            out = [None] * 19
            out[0] = post[0, x] + WEIGHTS[0] * flat
            for i in range(1, 19, 2):
                a = along(i, v)
                even = WEIGHTS[i] * flat + (4.5 * WEIGHTS[i]) * rho * (a * a)
                odd = (3.0 * WEIGHTS[i]) * rho * a
                out[i] = post[i, x] + even + odd
                out[i + 1] = post[i + 1, x] + even - odd
            for i in range(19):
                post[i, x] = out[i]
            for s in SIGNS:
                if x == (X - 1 if s == 1 else 0):
                    for slot, i in enumerate(CROSS[0][s]):
                        ax[INDEX[s], slot] = out[i]
                y = Y - 1 if s == 1 else 0
                for slot, i in enumerate(CROSS[1][s]):
                    ay[INDEX[s], slot, 1 + x : 2 + x, :] = out[i][y : y + 1, :]
            if place == 1:
                early = []
                for s in SIGNS:
                    early.append((ax.at[INDEX[s]], rax.at[INDEX[s]], (s, 0, 0)))
                for e, (a, b) in enumerate(EDGES):
                    ae[e] = post[DIRS.index((a, b, 0)), xsrc(a)][ysrc(b) : ysrc(b) + 1, :]
                    ae[4 + e] = to_row(post[DIRS.index((a, 0, b)), xsrc(a)], zsrc(b))
                    early.append((ae.at[e], rae.at[e], (a, b, 0)))
                    early.append((ae.at[4 + e], rae.at[4 + e], (a, 0, b)))
                flying = run(early, sa, ra)

        messages = []
        for e, (a, b) in enumerate(EDGES):
            i = DIRS.index((0, a, b))
            ae[8 + e] = corners([post[i, x] for x in range(X)], a, b)
            messages.append((ae.at[8 + e], rae.at[8 + e], (0, a, b)))
        for s in SIGNS:
            messages.append((ay.at[INDEX[s]], ray.at[INDEX[s]], (0, s, 0)))
        flying = flying + run(messages, sa, ra, len(flying))
        messages = []
        for s in SIGNS:
            az[INDEX[s]] = pack(
                [[(post[i, x], Z - 1 if s == 1 else 0) for x in range(X)] for i in CROSS[2][s]], s
            )
            messages.append((az.at[INDEX[s]], raz.at[INDEX[s]], (0, 0, s)))
        flying = flying + run(messages, sa, ra, len(flying))
        finish(flying)

        flows = {}
        flying = []
        for place, x in enumerate(outer_first):
            ps = []
            for i, (cx, cy, cz) in enumerate(DIRS):
                xs = x - cx
                own = 0 <= xs < X
                p = post[i, xs] if own else rax[INDEX[cx], CROSS[0][cx].index(i)]
                if cz:
                    at = CROSS[2][cz].index(i) * LANES + 1
                    if own:
                        p = zshift(p, cz, raz[INDEX[cz]], at + xs)
                    else:
                        p = zinsert(p, cz, to_col(rae[4 + edge[(cx, cz)]], lane, row), lane)
                if cy:
                    if own:
                        halo = ray[INDEX[cy], CROSS[1][cy].index(i), 1 + xs : 2 + xs, :]
                    else:
                        halo = rae[edge[(cx, cy)]]
                    if cz:
                        cell = roll(rae[8 + edge[(cy, cz)]], zend(cz) - (1 + x), 1)
                        halo = jnp.where(lane1 == zend(cz), cell, roll(halo, cz, 1))
                    p = yshift(p, cy, halo)
                pops[i, x] = p
                ps.append(p)
            rho, moms = moments(ps)
            inv = 1.0 / rho
            flows[x] = [m * inv for m in moms]
            if place == 1:
                early = []
                for s in SIGNS:
                    cx_[INDEX[s]] = flows[xsrc(s)][0]
                    early.append((cx_.at[INDEX[s]], rcx.at[INDEX[s]], (s, 0, 0)))
                flying = run(early, sc, rc)

        for s in SIGNS:
            si = INDEX[s]
            y = Y - 1 if s == 1 else 0
            for x in range(X):
                cy_[si, 1 + x : 2 + x, :] = flows[x][1][y : y + 1, :]
            cz_[si] = pack([[(flows[x][2], Z - 1 if s == 1 else 0) for x in range(X)]], s)
        messages = []
        for s in SIGNS:
            si = INDEX[s]
            messages.append((cy_.at[si], rcy.at[si], (0, s, 0)))
            messages.append((cz_.at[si], rcz.at[si], (0, 0, s)))
        finish(flying + run(messages, sc, rc, len(flying)))

        for x in range(X):
            f, pair = flows[x], pairs[x]
            fx_up = flows[x + 1][0] if x + 1 < X else rcx[1]
            fx_dn = flows[x - 1][0] if x > 0 else rcx[0]
            change = (f[0] + fx_up) * pair[(0, -1)] - (f[0] + fx_dn) * pair[(0, 1)]
            for s in SIGNS:
                fy = yshift(f[1], s, rcy[INDEX[s], 1 + x : 2 + x, :])
                fz = zshift(f[2], s, rcz[INDEX[s]], 1 + x)
                part = (f[1] + fy) * pair[(1, s)] + (f[2] + fz) * pair[(2, s)]
                change = change - part if s == 1 else change + part
            order[x] = O[x] - (0.25 * change - mobility * diffused[x])
        return carry

    lax.fori_loop(0, ITERS, step, 0)


def on_device(sizes, order_param, density, velocity):
    X, Y, Z = order_param.shape
    f32 = jnp.float32
    plane, rows = (Y, Z), (8, Z)
    vmem = [
        (19, X, Y, Z),
        (2, 5) + plane, (2, 5) + rows, (2,) + plane,
        (2, 5) + plane, (2, 5) + rows, (2,) + plane,
        (12, 1, Z), (12, 1, Z),
        (2, 2) + rows, (2,) + plane,
        (2, 2) + plane, (2, 2) + rows, (2,) + plane,
        (12, 1, Z), (12, 1, Z),
        (2,) + plane, (2,) + rows, (2,) + plane,
        (2,) + plane, (2,) + rows, (2,) + plane,
    ]
    sems = [18, 18, 18, 18, 6, 6]
    spec = pl.BlockSpec(memory_space=pltpu.VMEM)
    return pl.pallas_call(
        functools.partial(kernel, sizes),
        out_shape=(
            jax.ShapeDtypeStruct((X, Y, Z), f32),
            jax.ShapeDtypeStruct((19, X, Y, Z), f32),
        ),
        in_specs=[spec] * 3,
        out_specs=(spec, spec),
        scratch_shapes=[pltpu.VMEM(s, f32) for s in vmem]
        + [pltpu.SemaphoreType.DMA((n,)) for n in sems],
        compiler_params=pltpu.CompilerParams(collective_id=0, has_side_effects=True),
    )(order_param, density, velocity)


def solution(mesh):
    sizes = tuple(mesh.shape[a] for a in ("gx", "gy", "gz"))
    return jax.shard_map(
        functools.partial(on_device, sizes),
        mesh=mesh,
        in_specs=(P("gx", "gy", "gz"), P("gx", "gy", "gz"), P(None, "gx", "gy", "gz")),
        out_specs=(P("gx", "gy", "gz"), P(None, "gx", "gy", "gz")),
        check_vma=False,
    )
```

profile of v0, /device:TPU:0, one launch (start us, length us, event | category | flops | bytes accessed | tf_op | source)
XLA Modules:
  0.0 76.3 jit_solution(1822268335991525031)
XLA Ops:
  0.6 72.3 %shard_map.50 = (f32[4,16,128]{2,1,0:T(8,128)}, f32[19,4,16,128]{3,2,1,0:T(8,128)}) custom-call(f32[4,16,128]{2,1,0:T(8,128)} %order_in.1, f32[4,16,128]{2,1,0:T(8,128)} %dens_in.1, f32[3,4,16,128]{3,2,1,0:T(8,128)} %vel_in.1), custom_call_target="tpu_custom_call" | custom-call | tf_op jit(solution)/shard_map/pallas_call | solution.py:445
  72.9 1.4 %copy.7 = f32[4,16,128]{2,1,0:T(8,128)} copy(f32[4,16,128]{2,1,0:T(8,128)} %get-tuple-element.4) | data formatting | bytes 65536
  74.3 2.0 %copy.8 = f32[19,4,16,128]{3,2,1,0:T(8,128)} copy(f32[19,4,16,128]{3,2,1,0:T(8,128)} %get-tuple-element.5) | data formatting | bytes 1245184
where the time goes:
time: 76.5 us; the launch traced here: 76.3 us
  Pallas kernels  72.3 us (95%)
  local copies, waits for them, and re-layouts  3.33 us (4%)
    pallas_call x1, Pallas kernels, on_device(): pl.pallas_call(functools.partial(kernel, sizes), out_shape=(jax.ShapeDtyp...  72.3 us
    unnamed x2, local copies, waits for them, and re-layouts  3.33 us

commit v1 on v0

v1 whole, which is shorter than its diff:
```python
import functools

import jax
import jax.numpy as jnp
from jax import lax
from jax.experimental import pallas as pl
from jax.experimental.pallas import tpu as pltpu
from jax.sharding import PartitionSpec as P

ITERS = 5
MESH = pl.DeviceIdType.MESH
AXES = ("gx", "gy", "gz")
DIRS = [
    (0, 0, 0),
    (1, 0, 0),
    (-1, 0, 0),
    (0, 1, 0),
    (0, -1, 0),
    (0, 0, 1),
    (0, 0, -1),
    (1, 1, 0),
    (-1, -1, 0),
    (1, -1, 0),
    (-1, 1, 0),
    (1, 0, 1),
    (-1, 0, -1),
    (1, 0, -1),
    (-1, 0, 1),
    (0, 1, 1),
    (0, -1, -1),
    (0, 1, -1),
    (0, -1, 1),
]
WEIGHTS = [1.0 / 3.0] + [1.0 / 18.0] * 6 + [1.0 / 36.0] * 12
quadratic = -0.1
quartic = 0.1
stiffness = 0.02
mobility = 0.5
relax_time = 0.8

SIGNS = (1, -1)
INDEX = {1: 0, -1: 1}
TRAVEL = {0: 0, 1: 1, -1: 2}
CROSS = [{s: [i for i in range(19) if DIRS[i][d] == s] for s in SIGNS} for d in range(3)]
EDGES = [(a, b) for a in SIGNS for b in SIGNS]
ZPAIRS = [
    (DIRS.index((a, b, 1)), DIRS.index((a, b, -1)))
    for a, b in ((0, 0), (1, 0), (-1, 0), (0, 1), (0, -1))
]
LANES = 8
DEEP = 3
HALF = 64
MOMS = 4


def kernel(sizes, order_in, dens_in, vel_in, order, pops, *scratch):
    (post, mom, sx, rx, rxo, sy, ry, sz, fz, fy, fl) = scratch[0:11]
    (cx_, cy_, cz_, rcx, rcy, rcz) = scratch[11:17]
    (sa, ra, sc, rc) = scratch[17:21]
    X, Y, Z = order.shape
    E = Y + 16
    own_rows = slice(8, 8 + Y)
    block = 2 * DEEP
    width = X * block
    me = [lax.axis_index(a) for a in AXES]
    zsides = (1,) if sizes[2] == 2 else SIGNS

    def device(off):
        return {
            a: lax.rem(me[k] + (off[k] + sizes[k]), sizes[k]) if off[k] else me[k]
            for k, a in enumerate(AXES)
        }

    partners = [
        (a, b, c)
        for a in (0, 1, -1)
        for b in (0, 1, -1)
        for c in (0, 1, -1)
        if (a, b, c) != (0, 0, 0)
    ]
    barrier = pltpu.get_barrier_semaphore()
    for off in partners:
        pl.semaphore_signal(barrier, inc=1, device_id=device(off), device_id_type=MESH)

    lane = lax.broadcasted_iota(jnp.int32, (Y, Z), 1)
    row = lax.broadcasted_iota(jnp.int32, (Y, Z), 0)
    elane = lax.broadcasted_iota(jnp.int32, (E, Z), 1)
    left = elane < HALF
    frame = jnp.where(left, elane, elane - HALF)
    inner = lax.rem(frame, block) < DEEP
    zsign = jnp.where(left, 1.0, -1.0)
    low_col = lane < HALF

    def roll(v, s, axis):
        s = s % v.shape[axis]
        return v if s == 0 else pltpu.roll(v, s, axis)

    def zend(s):
        return 0 if s == 1 else Z - 1

    def yend(s):
        return 0 if s == 1 else Y - 1

    def xsrc(s):
        return X - 1 if s == 1 else 0

    def ysrc(s):
        return Y - 1 if s == 1 else 0

    def ybase(s):
        return 4 if s == 1 else 0

    def zat(px, s):
        return (px + DEEP) * block + (DEEP - 1 if s == 1 else HALF + DEEP)

    def zshift(v, s, packed, at):
        lanes = lane if v.shape[0] == Y else elane
        col = roll(packed, zend(s) - at, 1)
        return jnp.where(lanes == zend(s), col, roll(v, s, 1))

    def yshift(v, s, halo):
        return jnp.where(row == yend(s), jnp.broadcast_to(halo, v.shape), roll(v, s, 0))

    def pack(planes, s):
        acc = jnp.zeros((Y, Z), jnp.float32)
        for x in range(X):
            at = 1 + x
            acc = jnp.where(lane == at, roll(planes[x], at - (Z - 1 if s == 1 else 0), 1), acc)
        return acc

    def run(messages, ssem, rsem, first=0):
        copies = []
        for k, (src, dst, off) in enumerate(messages, first):
            copy = pltpu.make_async_remote_copy(
                src_ref=src,
                dst_ref=dst,
                send_sem=ssem.at[k],
                recv_sem=rsem.at[k],
                device_id=device(off),
                device_id_type=MESH,
            )
            copy.start()
            copies.append(copy)
        return copies

    def finish(copies):
        for copy in copies:
            copy.wait_recv()
        for copy in copies:
            copy.wait_send()

    def moments(ps):
        rho = ps[0]
        for i in range(1, 19):
            rho = rho + ps[i]
        moms = []
        for d in range(3):
            up = functools.reduce(lambda a, b: a + b, [ps[i] for i in CROSS[d][1]])
            down = functools.reduce(lambda a, b: a + b, [ps[i] for i in CROSS[d][-1]])
            moms.append(up - down)
        return rho, moms

    def chemical(o, beside):
        return quadratic * o + quartic * o * o * o - stiffness * (beside - 6.0 * o)

    def along(i, w):
        a = None
        for d in range(3):
            if DIRS[i][d]:
                t = w[d] if DIRS[i][d] == 1 else -w[d]
                a = t if a is None else a + t
        return a

    keep = 1.0 - 1.0 / relax_time
    mix = 1.0 / relax_time - 1.0

    def relaxed(x, ps, rho, u):
        flat = (mix * rho) * (1.0 - 1.5 * (u[0] * u[0] + u[1] * u[1] + u[2] * u[2]))
        out = [keep * ps[0] + WEIGHTS[0] * flat]
        for i in range(1, 19, 2):
            a = along(i, u)
            even = WEIGHTS[i] * flat + (4.5 * mix * WEIGHTS[i]) * rho * (a * a)
            odd = (3.0 * mix * WEIGHTS[i]) * rho * a
            out.append(keep * ps[i] + even + odd)
            out.append(keep * ps[i + 1] + even - odd)
        return out

    def place(acc, v, slot, x):
        at = slot * width + x * block
        mask = (lane >= at) & (lane < at + block)
        return jnp.where(mask, roll(v, at - (Z - DEEP), 1), acc)

    def ready(x, ps, rho, u):
        out = relaxed(x, ps, rho, u)
        heads = [rho] + u
        for i in range(19):
            post[i, x] = out[i]
        for g in range(MOMS):
            mom[g, x] = heads[g]
        for s in SIGNS:
            if x == xsrc(s):
                for g in range(MOMS):
                    sx[INDEX[s], g] = heads[g]
                for k, i in enumerate(CROSS[0][s]):
                    sx[INDEX[s], MOMS + k] = out[i]
            y, at = ysrc(s), ybase(s) + x
            for g in range(MOMS):
                sy[INDEX[s], 3 + X + g, at : at + 1, :] = heads[g][y : y + 1, :]
            for k, i in enumerate(CROSS[1][s]):
                sy[INDEX[s], 3 + X + MOMS + k, at : at + 1, :] = out[i][y : y + 1, :]
        first = sz[0]
        for g in range(MOMS):
            first = place(first, heads[g], 1 + g, x)
        sz[0] = first
        second = sz[1]
        for k, (up, down) in enumerate(ZPAIRS):
            second = place(second, jnp.where(low_col, out[down], out[up]), k, x)
        sz[1] = second

    def forced(rho, inv, u, force):
        v = [u[d] + force[d] * inv for d in range(3)]
        flat = rho * (1.0 - 1.5 * (v[0] * v[0] + v[1] * v[1] + v[2] * v[2]))
        return v, flat

    def one(i, rho, a, flat):
        return WEIGHTS[i] * (flat + rho * (a * (3.0 + 4.5 * a)))

    for ref in (sy, cy_, sz):
        ref[...] = jnp.zeros_like(ref)

    for x in range(X):
        order[x] = order_in[x]
        r = dens_in[x]
        u = [vel_in[d, x] for d in range(3)]
        usq = 1.0 - 1.5 * (u[0] * u[0] + u[1] * u[1] + u[2] * u[2])
        ps = []
        for i in range(19):
            a = along(i, u)
            if a is None:
                ps.append(WEIGHTS[i] * r * usq)
            else:
                ps.append(WEIGHTS[i] * r * (usq + 3.0 * a + 4.5 * a * a))
        rho, moms = moments(ps)
        inv = 1.0 / rho
        ready(x, ps, rho, [m * inv for m in moms])
    pl.semaphore_wait(barrier, len(partners))

    outer_first = sorted(range(X), key=lambda x: (min(x, X - 1 - x), x))

    def step(n, carry):
        par = lax.rem(n, 2)
        O = [order[x] for x in range(X)]
        for x in range(X):
            for s in SIGNS:
                sy[INDEX[s], 3 + x] = O[x][Y - 8 :, :] if s == 1 else O[x][:8, :]
        first = sz[0]
        for x in range(X):
            first = place(first, O[x], 0, x)
        sz[0] = first

        messages = []
        for c in zsides:
            for b in (1, -1, 0):
                for a in (1, -1, 0):
                    dst = fz.at[par, INDEX[c], TRAVEL[a]]
                    if b == 0:
                        src, dst = sz, dst.at[:, pl.ds(8, Y), :]
                    elif b == 1:
                        src, dst = sz.at[:, pl.ds(Y - 4, 4), :], dst.at[:, pl.ds(4, 4), :]
                    else:
                        src, dst = sz.at[:, pl.ds(0, 4), :], dst.at[:, pl.ds(8 + Y, 4), :]
                    messages.append((src, dst, (a, b, c)))
        for s in SIGNS:
            si = INDEX[s]
            rows = pl.ds(ybase(s), 4)
            span = pl.ds(3, X + MOMS + 5)
            messages.append((sy.at[si, span, rows, :], ry.at[par, si, span, rows, :], (0, s, 0)))
        for a, b in EDGES:
            bi = INDEX[b]
            rows = pl.ds(ybase(b), 4)
            src = pl.ds(3 + X - 3 if a == 1 else 3, 3)
            dst = pl.ds(0 if a == 1 else 3 + X + MOMS + 5, 3)
            messages.append((sy.at[bi, src, rows, :], ry.at[par, bi, dst, rows, :], (a, b, 0)))
            span = pl.ds(3 + X, MOMS + 5)
            src = pl.ds(ybase(b) + xsrc(a), 1)
            dst = pl.ds((ybase(b) + (-1 if a == 1 else X)) % 8, 1)
            messages.append((sy.at[bi, span, src, :], ry.at[par, bi, span, dst, :], (a, b, 0)))
        for s in SIGNS:
            si = INDEX[s]
            planes = order.at[pl.ds(X - 3, 3)] if s == 1 else order.at[pl.ds(0, 3)]
            messages.append((planes, rxo.at[par, si], (s, 0, 0)))
            messages.append((sx.at[si], rx.at[par, si], (s, 0, 0)))
        flying = run(messages, sa, ra.at[par])
        finish(flying)

        OE = {}
        for px in range(-DEEP, X + DEEP):
            if px < 0:
                mid, at = rxo[par, 0, px + DEEP], px + DEEP
            elif px >= X:
                mid, at = rxo[par, 1, px - X], 3 + X + MOMS + 5 + px - X
            else:
                mid, at = O[px], 3 + px
            OE[px] = jnp.concatenate([ry[par, 0, at], mid, ry[par, 1, at]], axis=0)

        def far(slot):
            plane, off = slot // 5, (slot % 5) * width
            base = DEEP * block
            out = []
            for c in zsides:
                parts = [fz[par, INDEX[c], TRAVEL[a], plane] for a in (0, 1, -1)]
                v = roll(parts[0], base - off, 1)
                v = jnp.where(frame < base, roll(parts[1], base - width - off, 1), v)
                v = jnp.where(frame >= base + width, roll(parts[2], base + width - off, 1), v)
                out.append(v)
            return out

        def far2(slot):
            plane, off = slot // 5, (slot % 5) * width
            base = DEEP * block
            halves = []
            for k, c in enumerate(zsides):
                parts = [fz[par, INDEX[c], TRAVEL[a], plane] for a in (0, 1, -1)]
                add = HALF * k
                v = roll(parts[0], base - off + add, 1)
                v = jnp.where(frame < base, roll(parts[1], base - width - off + add, 1), v)
                v = jnp.where(frame >= base + width, roll(parts[2], base + width - off + add, 1), v)
                halves.append(v)
            if len(halves) == 1:
                halves.append(roll(halves[0], HALF, 1))
            return jnp.where(left, halves[0], halves[1])

        near = jnp.zeros((E, Z), jnp.float32)
        for px in range(-DEEP, X + DEEP):
            at = (px + DEEP) * block
            mask = (elane >= at) & (elane < at + block)
            near = jnp.where(mask, roll(OE[px], at - (Z - DEEP), 1), near)
        near = jnp.where(left, near, roll(near, HALF, 1))
        OZ = jnp.where(left == inner, far2(0), near)

        C, pairs = {}, []
        for px in range(-2, X + 2):
            o = OE[px]
            around = {
                (0, 1): OE[px - 1],
                (0, -1): OE[px + 1],
                (1, 1): roll(o, 1, 0),
                (1, -1): roll(o, -1, 0),
                (2, 1): zshift(o, 1, OZ, zat(px, 1)),
                (2, -1): zshift(o, -1, OZ, zat(px, -1)),
            }
            C[px] = chemical(o, functools.reduce(lambda a, b: a + b, around.values()))
            if 0 <= px < X:
                pairs.append({k: O[px] + v[own_rows, :] for k, v in around.items()})
        beside = roll(OZ, 1, 0) + roll(OZ, -1, 0) + roll(OZ, 1, 1) + roll(OZ, -1, 1)
        beside = beside + roll(OZ, block, 1) + roll(OZ, -block, 1)
        CZ = chemical(OZ, beside)

        F, diffused = {}, []
        for px in range(-1, X + 1):
            c = C[px]
            y_dn, y_up = roll(c, 1, 0), roll(c, -1, 0)
            z_dn, z_up = zshift(c, 1, CZ, zat(px, 1)), zshift(c, -1, CZ, zat(px, -1))
            scale = -0.5 * OE[px]
            F[px] = [
                scale * (C[px + 1] - C[px - 1]),
                scale * (y_up - y_dn),
                scale * (z_up - z_dn),
            ]
            if 0 <= px < X:
                lap = C[px + 1] + C[px - 1] + y_up + y_dn + z_up + z_dn - 6.0 * c
                diffused.append(lap[own_rows, :])
            for s in SIGNS:
                at = (ybase(s) + px) % 8
                y = 7 if s == 1 else 8 + Y
                for d in range(3):
                    fy[INDEX[s], d, at : at + 1, :] = F[px][d][y : y + 1, :]
        scale = -0.5 * OZ
        FZ = [
            scale * (roll(CZ, -block, 1) - roll(CZ, block, 1)),
            scale * (roll(CZ, -1, 0) - roll(CZ, 1, 0)),
            scale * (roll(CZ, -1, 1) - roll(CZ, 1, 1)),
        ]

        XH, YH, ZH = {}, {}, {}
        for s in SIGNS:
            si = INDEX[s]
            rho = rx[par, si, 0]
            u = [rx[par, si, 1 + d] for d in range(3)]
            px = -1 if s == 1 else X
            v, flat = forced(rho, 1.0 / rho, u, [f[own_rows, :] for f in F[px]])
            for k, i in enumerate(CROSS[0][s]):
                XH[i] = rx[par, si, MOMS + k] + one(i, rho, along(i, v), flat)
            g = 3 + X
            rho = ry[par, si, g]
            u = [ry[par, si, g + 1 + d] for d in range(3)]
            v, flat = forced(rho, 1.0 / rho, u, [fy[si, d] for d in range(3)])
            for k, i in enumerate(CROSS[1][s]):
                YH[i] = ry[par, si, g + MOMS + k] + one(i, rho, along(i, v), flat)
        rho = far2(1)
        u = [far2(2 + d) for d in range(3)]
        v, flat = forced(rho, 1.0 / rho, u, FZ)
        for k, (up, down) in enumerate(ZPAIRS):
            a = zsign * v[2]
            for d in range(2):
                if DIRS[up][d]:
                    a = a + v[d] if DIRS[up][d] == 1 else a - v[d]
            h = far2(5 + k) + one(up, rho, a, flat)
            h = roll(h, DIRS[up][1], 0)[own_rows, :]
            ZH[up] = ZH[down] = h

        for x in range(X):
            rho = mom[0, x]
            u = [mom[1 + d, x] for d in range(3)]
            v, flat = forced(rho, 1.0 / rho, u, [f[own_rows, :] for f in F[x]])
            post[0, x] = post[0, x] + WEIGHTS[0] * flat
            for i in range(1, 19, 2):
                a = along(i, v)
                even = WEIGHTS[i] * flat + (4.5 * WEIGHTS[i]) * rho * (a * a)
                odd = (3.0 * WEIGHTS[i]) * rho * a
                post[i, x] = post[i, x] + even + odd
                post[i + 1, x] = post[i + 1, x] + even - odd

        flows = {}
        for x in outer_first:
            ps = []
            for i, (cx, cy, cz) in enumerate(DIRS):
                xs = x - cx
                p = post[i, xs] if 0 <= xs < X else XH[i]
                if cy:
                    at = (ybase(cy) + xs) % 8
                    p = yshift(p, cy, YH[i][at : at + 1, :])
                if cz:
                    p = zshift(p, cz, ZH[i], zat(xs, cz))
                pops[i, x] = p
                ps.append(p)
            rho, moms = moments(ps)
            inv = 1.0 / rho
            flows[x] = [m * inv for m in moms]
            mom[0, x] = rho
            for s in SIGNS:
                if x == xsrc(s):
                    cx_[INDEX[s]] = flows[x][0]
                y = ysrc(s)
                cy_[INDEX[s], 1 + x : 2 + x, :] = flows[x][1][y : y + 1, :]
        messages = []
        for s in SIGNS:
            messages.append((cy_.at[INDEX[s]], rcy.at[INDEX[s]], (0, s, 0)))
        for s in SIGNS:
            cz_[INDEX[s]] = pack([flows[x][2] for x in range(X)], s)
            messages.append((cz_.at[INDEX[s]], rcz.at[INDEX[s]], (0, 0, s)))
        for s in SIGNS:
            messages.append((cx_.at[INDEX[s]], rcx.at[INDEX[s]], (s, 0, 0)))
        flying = run(messages, sc, rc)

        for x in range(X):
            ready(x, [pops[i, x] for i in range(19)], mom[0, x], flows[x])
        finish(flying)

        for x in range(X):
            f, pair = flows[x], pairs[x]
            fx_up = flows[x + 1][0] if x + 1 < X else rcx[1]
            fx_dn = flows[x - 1][0] if x > 0 else rcx[0]
            change = (f[0] + fx_up) * pair[(0, -1)] - (f[0] + fx_dn) * pair[(0, 1)]
            for s in SIGNS:
                gy = yshift(f[1], s, rcy[INDEX[s], 1 + x : 2 + x, :])
                gz = zshift(f[2], s, rcz[INDEX[s]], 1 + x)
                part = (f[1] + gy) * pair[(1, s)] + (f[2] + gz) * pair[(2, s)]
                change = change - part if s == 1 else change + part
            order[x] = O[x] - (0.25 * change - mobility * diffused[x])
        return carry

    lax.fori_loop(0, ITERS, step, 0)


def on_device(sizes, order_param, density, velocity):
    X, Y, Z = order_param.shape
    f32 = jnp.float32
    plane, rows, tall = (Y, Z), (8, Z), (Y + 16, Z)
    tiles = X + 6 + MOMS + 5
    vmem = [
        (19, X, Y, Z), (MOMS, X, Y, Z),
        (2, MOMS + 5) + plane, (2, 2, MOMS + 5) + plane, (2, 2, 3) + plane,
        (2, tiles) + rows, (2, 2, tiles) + rows,
        (2,) + plane, (2, 2, 3, 2) + tall,
        (2, 3) + rows, (8, Z),
        (2,) + plane, (2,) + rows, (2,) + plane,
        (2,) + plane, (2,) + rows, (2,) + plane,
    ]
    count = (9 if sizes[2] == 2 else 18) + 14
    sems = [(count,), (2, count), (6,), (6,)]
    spec = pl.BlockSpec(memory_space=pltpu.VMEM)
    return pl.pallas_call(
        functools.partial(kernel, sizes),
        out_shape=(
            jax.ShapeDtypeStruct((X, Y, Z), f32),
            jax.ShapeDtypeStruct((19, X, Y, Z), f32),
        ),
        in_specs=[spec] * 3,
        out_specs=(spec, spec),
        scratch_shapes=[pltpu.VMEM(s, f32) for s in vmem]
        + [pltpu.SemaphoreType.DMA(n) for n in sems],
        compiler_params=pltpu.CompilerParams(collective_id=0, has_side_effects=True),
    )(order_param, density, velocity)


def solution(mesh):
    sizes = tuple(mesh.shape[a] for a in AXES)
    return jax.shard_map(
        functools.partial(on_device, sizes),
        mesh=mesh,
        in_specs=(P("gx", "gy", "gz"), P("gx", "gy", "gz"), P(None, "gx", "gy", "gz")),
        out_specs=(P("gx", "gy", "gz"), P(None, "gx", "gy", "gz")),
        check_vma=False,
    )
```

time: 76.5 us -> 64.8 us (0.85)
  Pallas kernels: 72.3 us -> 60.6 us
    pallas_call x1, Pallas kernels: 72.3 us -> 60.6 us  [on_device(): pl.pallas_call(functools.partial(kernel, sizes), out_shape=(jax.ShapeDtyp...]
where the time goes in v1:
time: 64.8 us; the launch traced here: 64.5 us
  Pallas kernels  60.6 us (94%)
  local copies, waits for them, and re-layouts  3.33 us (5%)
    pallas_call x1, Pallas kernels, on_device(): pl.pallas_call(functools.partial(kernel, sizes), out_shape=(jax.ShapeDtyp...  60.6 us
    unnamed x2, local copies, waits for them, and re-layouts  3.33 us

profile of v1, /device:TPU:0, one launch (start us, length us, event | category | flops | bytes accessed | tf_op | source)
XLA Modules:
  0.0 64.5 jit_solution(11988246999011767211)
XLA Ops:
  0.6 60.6 %shard_map.50 = (f32[4,16,128]{2,1,0:T(8,128)}, f32[19,4,16,128]{3,2,1,0:T(8,128)}) custom-call(f32[4,16,128]{2,1,0:T(8,128)} %order_in.1, f32[4,16,128]{2,1,0:T(8,128)} %dens_in.1, f32[3,4,16,128]{3,2,1,0:T(8,128)} %vel_in.1), custom_call_target="tpu_custom_call" | custom-call | tf_op jit(solution)/shard_map/pallas_call | solution.py:493
  61.2 1.4 %copy.7 = f32[4,16,128]{2,1,0:T(8,128)} copy(f32[4,16,128]{2,1,0:T(8,128)} %get-tuple-element.4) | data formatting | bytes 65536
  62.6 2.0 %copy.8 = f32[19,4,16,128]{3,2,1,0:T(8,128)} copy(f32[19,4,16,128]{3,2,1,0:T(8,128)} %get-tuple-element.5) | data formatting | bytes 1245184

commit v2 on v1

v2 whole, which is shorter than its diff:
```python
import functools

import jax
import jax.numpy as jnp
from jax import lax
from jax.experimental import pallas as pl
from jax.experimental.pallas import tpu as pltpu
from jax.sharding import PartitionSpec as P

ITERS = 5
MESH = pl.DeviceIdType.MESH
AXES = ("gx", "gy", "gz")
DIRS = [
    (0, 0, 0),
    (1, 0, 0),
    (-1, 0, 0),
    (0, 1, 0),
    (0, -1, 0),
    (0, 0, 1),
    (0, 0, -1),
    (1, 1, 0),
    (-1, -1, 0),
    (1, -1, 0),
    (-1, 1, 0),
    (1, 0, 1),
    (-1, 0, -1),
    (1, 0, -1),
    (-1, 0, 1),
    (0, 1, 1),
    (0, -1, -1),
    (0, 1, -1),
    (0, -1, 1),
]
WEIGHTS = [1.0 / 3.0] + [1.0 / 18.0] * 6 + [1.0 / 36.0] * 12
quadratic = -0.1
quartic = 0.1
stiffness = 0.02
mobility = 0.5
relax_time = 0.8

SIGNS = (1, -1)
INDEX = {1: 0, -1: 1}
TRAVEL = {0: 0, 1: 1, -1: 2}
CROSS = [{s: [i for i in range(19) if DIRS[i][d] == s] for s in SIGNS} for d in range(3)]
EDGES = [(a, b) for a in SIGNS for b in SIGNS]
ZPAIRS = [
    (DIRS.index((a, b, 1)), DIRS.index((a, b, -1)))
    for a, b in ((0, 0), (1, 0), (-1, 0), (0, 1), (0, -1))
]
DEEP = 3
HALF = 64
MOMS = 4


def kernel(sizes, order_in, dens_in, vel_in, order, pops, *scratch):
    (post, mom, base, oe, oz) = scratch[0:5]
    (sx, rx, sy, ry, rxy, sl, rl, sz, fz, fy) = scratch[5:15]
    (cx_, cy_, cz_, rcx, rcy, rcz) = scratch[15:21]
    (sa, ra, sc, rc) = scratch[21:25]
    X, Y, Z = order.shape
    E = Y + 16
    own_rows = slice(8, 8 + Y)
    block = 2 * DEEP
    width = X * block
    me = [lax.axis_index(a) for a in AXES]
    zsides = (1,) if sizes[2] == 2 else SIGNS

    def device(off):
        return {
            a: lax.rem(me[k] + (off[k] + sizes[k]), sizes[k]) if off[k] else me[k]
            for k, a in enumerate(AXES)
        }

    partners = [
        (a, b, c)
        for a in (0, 1, -1)
        for b in (0, 1, -1)
        for c in (0, 1, -1)
        if (a, b, c) != (0, 0, 0)
    ]
    barrier = pltpu.get_barrier_semaphore()
    for off in partners:
        pl.semaphore_signal(barrier, inc=1, device_id=device(off), device_id_type=MESH)

    lane = lax.broadcasted_iota(jnp.int32, (Y, Z), 1)
    row = lax.broadcasted_iota(jnp.int32, (Y, Z), 0)
    elane = lax.broadcasted_iota(jnp.int32, (E, Z), 1)
    erow = lax.broadcasted_iota(jnp.int32, (E, Z), 0)
    left = elane < HALF
    frame = jnp.where(left, elane, elane - HALF)
    column = lax.rem(frame, block)
    facing = lax.rem(elane, block) < DEEP
    zsign = jnp.where(left, 1.0, -1.0)
    low_col = lane < HALF
    face_z = column == DEEP
    face_x = (frame // block == DEEP) | (frame // block == DEEP + X)
    face_y = (erow == 8) | (erow == 8 + Y)
    below = jnp.where(erow == 8, 1.0, jnp.where(erow == 7, -1.0, 0.0))
    above = jnp.where(erow == 8 + Y, 1.0, jnp.where(erow == 7 + Y, -1.0, 0.0))

    def roll(v, s, axis):
        s = s % v.shape[axis]
        return v if s == 0 else pltpu.roll(v, s, axis)

    def zend(s):
        return 0 if s == 1 else Z - 1

    def yend(s):
        return 0 if s == 1 else Y - 1

    def xsrc(s):
        return X - 1 if s == 1 else 0

    def ysrc(s):
        return Y - 1 if s == 1 else 0

    def deep_rows(s):
        return pl.ds(8 - DEEP if s == 1 else 0, DEEP)

    def flat_rows(s):
        return pl.ds(0 if s == 1 else 4, X)

    def zat(px, s):
        return (px + DEEP) * block + (DEEP - 1 if s == 1 else HALF + DEEP)

    def zshift(v, s, packed, at):
        lanes = lane if v.shape[0] == Y else elane
        col = roll(packed, zend(s) - at, 1)
        return jnp.where(lanes == zend(s), col, roll(v, s, 1))

    def yshift(v, s, halo):
        return jnp.where(row == yend(s), jnp.broadcast_to(halo, v.shape), roll(v, s, 0))

    def pack(planes, s):
        acc = jnp.zeros((Y, Z), jnp.float32)
        for x in range(X):
            at = 1 + x
            acc = jnp.where(lane == at, roll(planes[x], at - (Z - 1 if s == 1 else 0), 1), acc)
        return acc

    def copies(messages, ssem, rsem):
        return [
            pltpu.make_async_remote_copy(
                src_ref=src,
                dst_ref=dst,
                send_sem=ssem.at[k],
                recv_sem=rsem.at[k],
                device_id=device(off),
                device_id_type=MESH,
            )
            for k, (src, dst, off) in enumerate(messages)
        ]

    def launch(flying):
        for copy in flying:
            copy.start()

    def finish(flying):
        for copy in flying:
            copy.wait_recv()
        for copy in flying:
            copy.wait_send()

    def bundle(par):
        messages = []
        for c in zsides:
            for b in (1, -1, 0):
                for a in (1, -1, 0):
                    dst = fz.at[par, INDEX[c], TRAVEL[a]]
                    rows = {1: pl.ds(Y - DEEP, DEEP), -1: pl.ds(0, DEEP), 0: pl.ds(0, Y)}[b]
                    land = {1: 8 - DEEP, -1: 8 + Y, 0: 8}[b]
                    land = pl.ds(land, DEEP if b else Y)
                    planes = pl.ds(0, 1 if a and b else 2)
                    messages.append((sz.at[planes, rows, :], dst.at[planes, land, :], (a, b, c)))
        for a, b in EDGES:
            bi, ai, rows = INDEX[b], INDEX[a], deep_rows(b)
            src = pl.ds(X - 1 if a == 1 else 0, 5)
            messages.append((sy.at[bi, src, rows, :], rxy.at[par, bi, ai, :, rows, :], (a, b, 0)))
            messages.append((sl.at[bi, ai], rl.at[par, bi, ai], (a, b, 0)))
        for s in SIGNS:
            si = INDEX[s]
            for span, rows in ((MOMS + 5, flat_rows(s)), (X + 4, deep_rows(s))):
                span = pl.ds(0, span)
                messages.append((sy.at[si, span, rows, :], ry.at[par, si, span, rows, :], (0, s, 0)))
        for s in SIGNS:
            messages.append((sx.at[INDEX[s]], rx.at[par, INDEX[s]], (s, 0, 0)))
        return copies(messages, sa, ra.at[par])

    def farewell():
        messages = []
        for s in SIGNS:
            messages.append((cy_.at[INDEX[s]], rcy.at[INDEX[s]], (0, s, 0)))
        for s in SIGNS:
            messages.append((cz_.at[INDEX[s]], rcz.at[INDEX[s]], (0, 0, s)))
        for s in SIGNS:
            messages.append((cx_.at[INDEX[s]], rcx.at[INDEX[s]], (s, 0, 0)))
        return copies(messages, sc, rc)

    def moments(ps):
        rho = ps[0]
        for i in range(1, 19):
            rho = rho + ps[i]
        moms = []
        for d in range(3):
            up = functools.reduce(lambda a, b: a + b, [ps[i] for i in CROSS[d][1]])
            down = functools.reduce(lambda a, b: a + b, [ps[i] for i in CROSS[d][-1]])
            moms.append(up - down)
        return rho, moms

    def chemical(o, beside):
        return quadratic * o + quartic * o * o * o - stiffness * (beside - 6.0 * o)

    def along(i, w):
        a = None
        for d in range(3):
            if DIRS[i][d]:
                t = w[d] if DIRS[i][d] == 1 else -w[d]
                a = t if a is None else a + t
        return a

    keep = 1.0 - 1.0 / relax_time
    mix = 1.0 / relax_time - 1.0

    def relaxed(ps, rho, u):
        flat = (mix * rho) * (1.0 - 1.5 * (u[0] * u[0] + u[1] * u[1] + u[2] * u[2]))
        out = [keep * ps[0] + WEIGHTS[0] * flat]
        for i in range(1, 19, 2):
            a = along(i, u)
            even = WEIGHTS[i] * flat + (4.5 * mix * WEIGHTS[i]) * rho * (a * a)
            odd = (3.0 * mix * WEIGHTS[i]) * rho * a
            out.append(keep * ps[i] + even + odd)
            out.append(keep * ps[i + 1] + even - odd)
        return out

    def place(acc, v, slot, x):
        at = slot * width + x * block
        mask = (lane >= at) & (lane < at + block)
        return jnp.where(mask, roll(v, at - (Z - DEEP), 1), acc)

    def ready():
        first = jnp.zeros((Y, Z), jnp.float32)
        second = jnp.zeros((Y, Z), jnp.float32)
        for x in range(X):
            rho = mom[0, x]
            u = [mom[1 + d, x] for d in range(3)]
            out = relaxed([pops[i, x] for i in range(19)], rho, u)
            heads, b = [rho] + u, base[x]
            for i in range(19):
                post[i, x] = out[i]
            for s in SIGNS:
                si = INDEX[s]
                if x == xsrc(s):
                    for g in range(MOMS):
                        sx[si, g] = heads[g]
                    for k, i in enumerate(CROSS[0][s]):
                        sx[si, MOMS + k] = out[i]
                slot = x - (X - DEEP) if s == 1 else x
                if 0 <= slot < DEEP:
                    sx[si, MOMS + 5 + slot] = b
                    sx[si, MOMS + 6 + DEEP, slot : slot + 1, :] = u[1][0:1, :]
                    sx[si, MOMS + 6 + DEEP, DEEP + slot : DEEP + slot + 1, :] = u[1][Y - 1 :, :]
                y, at = ysrc(s), (0 if s == 1 else 4) + x
                for g in range(MOMS):
                    sy[si, g, at : at + 1, :] = heads[g][y : y + 1, :]
                for k, i in enumerate(CROSS[1][s]):
                    sy[si, MOMS + k, at : at + 1, :] = out[i][y : y + 1, :]
                rows = slice(Y - DEEP, Y) if s == 1 else slice(0, DEEP)
                sy[si, 2 + x, deep_rows(s), :] = b[rows, :]
                if x == 0:
                    sy[si, 0, deep_rows(s), :] = u[0][rows, :]
                if x == X - 1:
                    sy[si, X + 3, deep_rows(s), :] = u[0][rows, :]
                for a in SIGNS:
                    if x == xsrc(a):
                        for k, v in enumerate(heads + [out[DIRS.index((a, s, 0))]]):
                            sl[si, INDEX[a], k : k + 1, :] = v[y : y + 1, :]
                    slot = x - (X - DEEP) if a == 1 else x - 1
                    if 0 <= slot < DEEP - 1:
                        sl[si, INDEX[a], 5 + slot : 6 + slot, :] = u[1][y : y + 1, :]
            for g, v in enumerate([b] + heads):
                first = place(first, v, g, x)
            for k, (up, down) in enumerate(ZPAIRS):
                second = place(second, jnp.where(low_col, out[down], out[up]), k, x)
        sz[0] = first
        sz[1] = second
        for s in SIGNS:
            si = INDEX[s]
            sx[si, MOMS + 5 + DEEP] = first
            rows = slice(Y - DEEP, Y) if s == 1 else slice(0, DEEP)
            for at in (1, X + 2):
                sy[si, at, deep_rows(s), :] = first[rows, :]

    def forced(rho, inv, u, force):
        v = [u[d] + force[d] * inv for d in range(3)]
        flat = rho * (1.0 - 1.5 * (v[0] * v[0] + v[1] * v[1] + v[2] * v[2]))
        return v, flat

    def one(i, rho, a, flat):
        return WEIGHTS[i] * (flat + rho * (a * (3.0 + 4.5 * a)))

    for ref in (sx, sy, sl, cy_, oe, oz):
        ref[...] = jnp.zeros_like(ref)

    for x in range(X):
        base[x] = order_in[x]
        r = dens_in[x]
        u = [vel_in[d, x] for d in range(3)]
        usq = 1.0 - 1.5 * (u[0] * u[0] + u[1] * u[1] + u[2] * u[2])
        ps = []
        for i in range(19):
            a = along(i, u)
            if a is None:
                ps.append(WEIGHTS[i] * r * usq)
            else:
                ps.append(WEIGHTS[i] * r * (usq + 3.0 * a + 4.5 * a * a))
            pops[i, x] = ps[i]
        rho, moms = moments(ps)
        inv = 1.0 / rho
        mom[0, x] = rho
        for d in range(3):
            mom[1 + d, x] = moms[d] * inv
    ready()
    pl.semaphore_wait(barrier, len(partners))
    launch(bundle(0))

    outer_first = sorted(range(X), key=lambda x: (min(x, X - 1 - x), x))

    def step(n, carry):
        par = lax.rem(n, 2)
        finish(bundle(par))
        low, high = ry.at[par, 0], ry.at[par, 1]

        def tall(a):
            if a == 0:
                near = [low[1], sz[0], high[1]]
            else:
                at = DEEP if a == 1 else 1
                mid = rx[par, INDEX[a], MOMS + 5 + DEEP]
                near = [rxy[par, 0, INDEX[a], at], mid, rxy[par, 1, INDEX[a], at]]
            near = jnp.concatenate(near, axis=0)
            far = [fz[par, INDEX[c], TRAVEL[a], 0] for c in zsides]
            halves = [jnp.where(facing, far[0], near), jnp.where(facing, near, far[-1])]
            return [roll(v, -a * width, 1) for v in halves]

        parts = [tall(a) for a in (0, 1, -1)]
        ends = [
            [roll(fz[par, INDEX[c], TRAVEL[a], 1], -a * width, 1) for a in (0, 1, -1)] for c in zsides
        ]

        def gather(three, slot, add):
            at = slot * width
            rel = lax.rem(elane + (Z - at), Z)
            v = jnp.where(rel < width, three[0], jnp.where(rel < HALF, three[2], three[1]))
            return roll(v, DEEP * block - at + add, 1)

        def packed(slot):
            halves = [gather([p[k] for p in parts], slot, HALF * k) for k in range(2)]
            return jnp.where(left, halves[0], halves[1])

        def packed_far(slot):
            halves = [gather(three, slot, HALF * k) for k, three in enumerate(ends)]
            if len(halves) == 1:
                halves.append(roll(halves[0], HALF, 1))
            return jnp.where(left, halves[0], halves[1])

        rho_z = packed(1)
        u_z = [packed(2 + d) for d in range(3)]
        old = oz[...]
        OZ = packed(0)
        for d, (shift, axis, mask) in enumerate(((block, 1, face_x), (1, 0, face_y), (1, 1, face_z))):
            t = 0.25 * (u_z[d] + roll(u_z[d], shift, axis)) * (old + roll(old, shift, axis))
            t = jnp.where(mask, t, 0.0)
            OZ = OZ + (t - roll(t, -shift, axis))
        oz[...] = OZ

        def around(px, s):
            if px < 0:
                return rxy[par, INDEX[s], 0, px + DEEP]
            if px >= X:
                return rxy[par, INDEX[s], 1, 2 + px - X]
            return ry[par, INDEX[s], 2 + px]

        def speed(px):
            if px < 0:
                tiles, mid = [rxy[par, k, 0, 4] for k in range(2)], rx[par, 0, 1]
            elif px >= X:
                tiles, mid = [rxy[par, k, 1, 0] for k in range(2)], rx[par, 1, 1]
            else:
                tiles, mid = [ry[par, k, 0 if px == 0 else X + 3] for k in range(2)], mom[1, px]
            return jnp.concatenate([tiles[0], mid, tiles[1]], axis=0)

        def outside(px, s):
            si = INDEX[s]
            if px < 0:
                at = 2 if px == -1 else 5 + px + DEEP
                return rl[par, si, 0, at : at + 1, :]
            if px >= X:
                at = 2 if px == X else 5 + px - X - 1
                return rl[par, si, 1, at : at + 1, :]
            at = (0 if s == 1 else 4) + px
            return ry[par, si, 2, at : at + 1, :]

        def inside(px, s):
            if 0 <= px < X:
                y = yend(s)
                return mom[2, px, y : y + 1, :]
            side, slot = (0, px + DEEP) if px < 0 else (1, px - X)
            at = slot if s == 1 else DEEP + slot
            return rx[par, side, MOMS + 6 + DEEP, at : at + 1, :]

        across = {}
        for lo, hi in ((-1, 0), (X - 1, X)):
            t = 0.25 * (speed(lo) + speed(hi)) * (oe[lo + DEEP] + oe[hi + DEEP])
            across[lo], across[hi] = -t, t
        OE = {}
        for px in range(-DEEP, X + DEEP):
            if px < 0:
                mid = rx[par, 0, MOMS + 5 + px + DEEP]
            elif px >= X:
                mid = rx[par, 1, MOMS + 5 + px - X]
            else:
                mid = base[px]
            v = jnp.concatenate([around(px, 1), mid, around(px, -1)], axis=0)
            if px in across:
                v = v + across[px]
            for s, sign, y in ((1, below, 8), (-1, above, 8 + Y)):
                pair = oe[px + DEEP, y - 1 : y, :] + oe[px + DEEP, y : y + 1, :]
                t = 0.25 * (outside(px, s) + inside(px, s)) * pair
                v = v + sign * jnp.broadcast_to(t, v.shape)
            at = (px + DEEP) * block
            v = jnp.where(elane == 0, roll(OZ, -(at + DEEP), 1), v)
            v = jnp.where(elane == Z - 1, roll(OZ, Z - 1 - (HALF + at + DEEP - 1), 1), v)
            OE[px] = v
        for px in range(-DEEP, X + DEEP):
            oe[px + DEEP] = OE[px]
        O = [OE[x][own_rows, :] for x in range(X)]

        C = {}
        for px in range(-2, X + 2):
            o = OE[px]
            beside = OE[px - 1] + OE[px + 1] + roll(o, 1, 0) + roll(o, -1, 0)
            beside = beside + zshift(o, 1, OZ, zat(px, 1)) + zshift(o, -1, OZ, zat(px, -1))
            C[px] = chemical(o, beside)
        beside = roll(OZ, 1, 0) + roll(OZ, -1, 0) + roll(OZ, 1, 1) + roll(OZ, -1, 1)
        beside = beside + roll(OZ, block, 1) + roll(OZ, -block, 1)
        CZ = chemical(OZ, beside)

        F = {}
        for px in range(-1, X + 1):
            c = C[px]
            y_dn, y_up = roll(c, 1, 0), roll(c, -1, 0)
            z_dn, z_up = zshift(c, 1, CZ, zat(px, 1)), zshift(c, -1, CZ, zat(px, -1))
            scale = -0.5 * OE[px]
            F[px] = [
                scale * (C[px + 1] - C[px - 1]),
                scale * (y_up - y_dn),
                scale * (z_up - z_dn),
            ]
            if 0 <= px < X:
                lap = C[px + 1] + C[px - 1] + y_up + y_dn + z_up + z_dn - 6.0 * c
                base[px] = O[px] + mobility * lap[own_rows, :]
                for s in SIGNS:
                    at = (0 if s == 1 else 4) + px
                    y = 7 if s == 1 else 8 + Y
                    for d in range(3):
                        fy[INDEX[s], d, at : at + 1, :] = F[px][d][y : y + 1, :]
        scale = -0.5 * OZ
        FZ = [
            scale * (roll(CZ, -block, 1) - roll(CZ, block, 1)),
            scale * (roll(CZ, -1, 0) - roll(CZ, 1, 0)),
            scale * (roll(CZ, -1, 1) - roll(CZ, 1, 1)),
        ]

        XH, YH, LH, ZH = {}, {}, {}, {}
        for s in SIGNS:
            si = INDEX[s]
            rho = rx[par, si, 0]
            u = [rx[par, si, 1 + d] for d in range(3)]
            px = -1 if s == 1 else X
            v, flat = forced(rho, 1.0 / rho, u, [f[own_rows, :] for f in F[px]])
            for k, i in enumerate(CROSS[0][s]):
                XH[i] = rx[par, si, MOMS + k] + one(i, rho, along(i, v), flat)
            rho = ry[par, si, 0]
            u = [ry[par, si, 1 + d] for d in range(3)]
            v, flat = forced(rho, 1.0 / rho, u, [fy[si, d] for d in range(3)])
            for k, i in enumerate(CROSS[1][s]):
                YH[i] = ry[par, si, MOMS + k] + one(i, rho, along(i, v), flat)
            for a in SIGNS:
                i = DIRS.index((a, s, 0))
                head = [rl[par, si, INDEX[a], k : k + 1, :] for k in range(5)]
                y, px = (7 if s == 1 else 8 + Y), (-1 if a == 1 else X)
                force = [f[y : y + 1, :] for f in F[px]]
                v, flat = forced(head[0], 1.0 / head[0], head[1:4], force)
                LH[i] = head[4] + one(i, head[0], along(i, v), flat)
        v, flat = forced(rho_z, 1.0 / rho_z, u_z, FZ)
        for k, (up, down) in enumerate(ZPAIRS):
            a = zsign * v[2]
            for d in range(2):
                if DIRS[up][d]:
                    a = a + v[d] if DIRS[up][d] == 1 else a - v[d]
            h = packed_far(k) + one(up, rho_z, a, flat)
            ZH[up] = ZH[down] = roll(h, DIRS[up][1], 0)[own_rows, :]

        for x in range(X):
            rho = mom[0, x]
            u = [mom[1 + d, x] for d in range(3)]
            v, flat = forced(rho, 1.0 / rho, u, [f[own_rows, :] for f in F[x]])
            post[0, x] = post[0, x] + WEIGHTS[0] * flat
            for i in range(1, 19, 2):
                a = along(i, v)
                even = WEIGHTS[i] * flat + (4.5 * WEIGHTS[i]) * rho * (a * a)
                odd = (3.0 * WEIGHTS[i]) * rho * a
                post[i, x] = post[i, x] + even + odd
                post[i + 1, x] = post[i + 1, x] + even - odd

        flows = {}
        for x in outer_first:
            ps = []
            for i, (cx, cy, cz) in enumerate(DIRS):
                xs = x - cx
                own = 0 <= xs < X
                p = post[i, xs] if own else XH[i]
                if cy:
                    at = (0 if cy == 1 else 4) + xs
                    p = yshift(p, cy, YH[i][at : at + 1, :] if own else LH[i])
                if cz:
                    p = zshift(p, cz, ZH[i], zat(xs, cz))
                pops[i, x] = p
                ps.append(p)
            rho, moms = moments(ps)
            inv = 1.0 / rho
            flows[x] = [m * inv for m in moms]
            mom[0, x] = rho
            for d in range(3):
                mom[1 + d, x] = flows[x][d]

        @pl.when(n == ITERS - 1)
        def _():
            for s in SIGNS:
                cx_[INDEX[s]] = mom[1, xsrc(s)]
                y = ysrc(s)
                for x in range(X):
                    cy_[INDEX[s], 1 + x : 2 + x, :] = mom[2, x, y : y + 1, :]
                cz_[INDEX[s]] = pack([mom[3, x] for x in range(X)], s)
            launch(farewell())

        tx = {0: 0.0, X: 0.0}
        for x in range(1, X):
            tx[x] = (flows[x][0] + flows[x - 1][0]) * (O[x] + O[x - 1])
        for x in range(X):
            f, o = flows[x], O[x]
            ty = jnp.where(row == 0, 0.0, (f[1] + roll(f[1], 1, 0)) * (o + roll(o, 1, 0)))
            tz = jnp.where(lane == 0, 0.0, (f[2] + roll(f[2], 1, 1)) * (o + roll(o, 1, 1)))
            change = tx[x + 1] - tx[x] + (roll(ty, -1, 0) - ty) + (roll(tz, -1, 1) - tz)
            base[x] = base[x] - 0.25 * change

        @pl.when(n < ITERS - 1)
        def _():
            ready()
            launch(bundle(1 - par))

        return carry

    lax.fori_loop(0, ITERS, step, 0)
    finish(farewell())

    OZ = oz[own_rows, :]
    for x in range(X):
        o, u = oe[x + DEEP, own_rows, :], [mom[1 + d, x] for d in range(3)]
        change = jnp.zeros((Y, Z), jnp.float32)
        if x == 0:
            change = change + (u[0] + rcx[0]) * (o + oe[DEEP - 1, own_rows, :])
        if x == X - 1:
            change = change - (u[0] + rcx[1]) * (o + oe[DEEP + X, own_rows, :])
        for s in SIGNS:
            at = 7 if s == 1 else 8 + Y
            other = rcy[INDEX[s], 1 + x : 2 + x, :]
            y = yend(s)
            t = (mom[2, x, y : y + 1, :] + other) * (
                oe[x + DEEP, at : at + 1, :] + oe[x + DEEP, 8 + y : 9 + y, :]
            )
            t = jnp.where(row == y, jnp.broadcast_to(t, (Y, Z)), 0.0)
            side = roll(OZ, zend(s) - zat(x, s), 1)
            beside = roll(rcz[INDEX[s]], zend(s) - (1 + x), 1)
            t = t + jnp.where(lane == zend(s), (u[2] + beside) * (o + side), 0.0)
            change = change + t if s == 1 else change - t
        order[x] = base[x] + 0.25 * change


def on_device(sizes, order_param, density, velocity):
    X, Y, Z = order_param.shape
    f32 = jnp.float32
    plane, rows, tall = (Y, Z), (8, Z), (Y + 16, Z)
    planes, tiles = MOMS + 5 + DEEP + 2, max(MOMS + 5, X + 4)
    vmem = [
        (19, X, Y, Z), (MOMS, X, Y, Z), (X, Y, Z), (X + 2 * DEEP,) + tall, tall,
        (2, planes) + plane, (2, 2, planes) + plane,
        (2, tiles) + rows, (2, 2, tiles) + rows, (2, 2, 2, 5) + rows,
        (2, 2) + rows, (2, 2, 2) + rows,
        (2,) + plane, (2, 2, 3, 2) + tall, (2, 3) + rows,
        (2,) + plane, (2,) + rows, (2,) + plane,
        (2,) + plane, (2,) + rows, (2,) + plane,
    ]
    count = (9 if sizes[2] == 2 else 18) + 14
    sems = [(count,), (2, count), (6,), (6,)]
    spec = pl.BlockSpec(memory_space=pltpu.VMEM)
    return pl.pallas_call(
        functools.partial(kernel, sizes),
        out_shape=(
            jax.ShapeDtypeStruct((X, Y, Z), f32),
            jax.ShapeDtypeStruct((19, X, Y, Z), f32),
        ),
        in_specs=[spec] * 3,
        out_specs=(spec, spec),
        scratch_shapes=[pltpu.VMEM(s, f32) for s in vmem]
        + [pltpu.SemaphoreType.DMA(n) for n in sems],
        compiler_params=pltpu.CompilerParams(collective_id=0, has_side_effects=True),
    )(order_param, density, velocity)


def solution(mesh):
    sizes = tuple(mesh.shape[a] for a in AXES)
    return jax.shard_map(
        functools.partial(on_device, sizes),
        mesh=mesh,
        in_specs=(P("gx", "gy", "gz"), P("gx", "gy", "gz"), P(None, "gx", "gy", "gz")),
        out_specs=(P("gx", "gy", "gz"), P(None, "gx", "gy", "gz")),
        check_vma=False,
    )
```

time: 64.8 us -> 52.3 us (0.81)
  Pallas kernels: 60.6 us -> 48 us
    pallas_call x1, Pallas kernels: 60.6 us -> 48 us  [on_device(): pl.pallas_call(functools.partial(kernel, sizes), out_shape=(jax.ShapeDtyp...]
where the time goes in v2:
time: 52.3 us; the launch traced here: 52 us
  Pallas kernels  48 us (92%)
  local copies, waits for them, and re-layouts  3.33 us (6%)
  between operations  0.64 us (1%)
    pallas_call x1, Pallas kernels, on_device(): pl.pallas_call(functools.partial(kernel, sizes), out_shape=(jax.ShapeDtyp...  48 us
    unnamed x2, local copies, waits for them, and re-layouts  3.33 us

profile of v2, /device:TPU:0, one launch (start us, length us, event | category | flops | bytes accessed | tf_op | source)
XLA Modules:
  0.0 52.0 jit_solution(17446889963156757763)
XLA Ops:
  0.6 48.0 %shard_map.50 = (f32[4,16,128]{2,1,0:T(8,128)}, f32[19,4,16,128]{3,2,1,0:T(8,128)}) custom-call(f32[4,16,128]{2,1,0:T(8,128)} %order_in.1, f32[4,16,128]{2,1,0:T(8,128)} %dens_in.1, f32[3,4,16,128]{3,2,1,0:T(8,128)} %vel_in.1), custom_call_target="tpu_custom_call" | custom-call | tf_op jit(solution)/shard_map/pallas_call | solution.py:607
  48.7 1.4 %copy.7 = f32[4,16,128]{2,1,0:T(8,128)} copy(f32[4,16,128]{2,1,0:T(8,128)} %get-tuple-element.4) | data formatting | bytes 65536
  50.1 2.0 %copy.8 = f32[19,4,16,128]{3,2,1,0:T(8,128)} copy(f32[19,4,16,128]{3,2,1,0:T(8,128)} %get-tuple-element.5) | data formatting | bytes 1245184

commit v3 on v2

--- a/solution.py
+++ b/solution.py
@@ -606,10 +606,7 @@
     spec = pl.BlockSpec(memory_space=pltpu.VMEM)
     return pl.pallas_call(
         functools.partial(kernel, sizes),
-        out_shape=(
-            jax.ShapeDtypeStruct((X, Y, Z), f32),
-            jax.ShapeDtypeStruct((19, X, Y, Z), f32),
-        ),
+        out_shape=(pltpu.VMEM((X, Y, Z), f32), pltpu.VMEM((19, X, Y, Z), f32)),
         in_specs=[spec] * 3,
         out_specs=(spec, spec),
         scratch_shapes=[pltpu.VMEM(s, f32) for s in vmem]

time: 52.3 us -> 49.5 us (0.946)
  local copies, waits for them, and re-layouts: 3.33 us -> 1.44 us
  Pallas kernels: 48 us -> 47.3 us
    unnamed x2, local copies, waits for them, and re-layouts: 3.33 us -> 1.44 us
    pallas_call x1, Pallas kernels: 48 us -> 47.3 us  [on_device(): pl.pallas_call(functools.partial(kernel, sizes), out_shape=(pltpu.VMEM((X...]
where the time goes in v3:
time: 49.5 us; the launch traced here: 49.4 us
  Pallas kernels  47.3 us (96%)
  local copies, waits for them, and re-layouts  1.44 us (3%)
  between operations  0.64 us (1%)
    pallas_call x1, Pallas kernels, on_device(): pl.pallas_call(functools.partial(kernel, sizes), out_shape=(pltpu.VMEM((X...  47.3 us
    unnamed x2, local copies, waits for them, and re-layouts  1.44 us

profile of v3, /device:TPU:0, one launch (start us, length us, event | category | flops | bytes accessed | tf_op | source)
XLA Modules:
  0.0 49.4 jit_solution(10824479367722245769)
XLA Ops:
  0.6 47.3 %shard_map.50 = (f32[4,16,128]{2,1,0:T(8,128)S(1)}, f32[19,4,16,128]{3,2,1,0:T(8,128)S(1)}) custom-call(f32[4,16,128]{2,1,0:T(8,128)} %order_in.1, f32[4,16,128]{2,1,0:T(8,128)} %dens_in.1, f32[3,4,16,128]{3,2,1,0:T(8,128)} %vel_in.1), custom_call_target="tpu_custom_call" | custom-call | tf_op jit(solution)/shard_map/pallas_call | solution.py:607
  47.9 0.6 %copy.7 = f32[4,16,128]{2,1,0:T(8,128)} copy(f32[4,16,128]{2,1,0:T(8,128)S(1)} %get-tuple-element.2) | data formatting | bytes 65536
  48.6 0.8 %copy.8 = f32[19,4,16,128]{3,2,1,0:T(8,128)} copy(f32[19,4,16,128]{3,2,1,0:T(8,128)S(1)} %get-tuple-element.3) | data formatting | bytes 1245184

commit v4 on v3

--- a/solution.py
+++ b/solution.py
@@ -1,4 +1,5 @@
 import functools
+import math
 
 import jax
 import jax.numpy as jnp
@@ -53,10 +54,10 @@
 
 
 def kernel(sizes, order_in, dens_in, vel_in, order, pops, *scratch):
-    (post, mom, base, oe, oz) = scratch[0:5]
-    (sx, rx, sy, ry, rxy, sl, rl, sz, fz, fy) = scratch[5:15]
-    (cx_, cy_, cz_, rcx, rcy, rcz) = scratch[15:21]
-    (sa, ra, sc, rc) = scratch[21:25]
+    (post, mom, base, oe, oz, dens, vel, bulk) = scratch[0:8]
+    (sx, rx, sy, ry, rxy, sz, fz, fy) = scratch[8:16]
+    (cx_, cy_, cz_, rcx, rcy, rcz) = scratch[16:22]
+    (si_, sa, ra, sc, rc) = scratch[22:27]
     X, Y, Z = order.shape
     E = Y + 16
     own_rows = slice(8, 8 + Y)
@@ -73,14 +74,23 @@
 
     partners = [
         (a, b, c)
-        for a in (0, 1, -1)
-        for b in (0, 1, -1)
-        for c in (0, 1, -1)
+        for a in (1, -1, 0)
+        for b in (1, -1, 0)
+        for c in zsides + (0,)
         if (a, b, c) != (0, 0, 0)
     ]
+    place_of = {off: device(off) for off in partners}
+    if sizes[2] == 2:
+        place_of[(0, 0, -1)] = place_of[(0, 0, 1)]
     barrier = pltpu.get_barrier_semaphore()
     for off in partners:
-        pl.semaphore_signal(barrier, inc=1, device_id=device(off), device_id_type=MESH)
+        pl.semaphore_signal(barrier, inc=1, device_id=place_of[off], device_id_type=MESH)
+    loads = [
+        pltpu.make_async_copy(src, dst, si_.at[k])
+        for k, (src, dst) in enumerate(((order_in, base), (dens_in, dens), (vel_in, vel)))
+    ]
+    for load in loads:
+        load.start()
 
     lane = lax.broadcasted_iota(jnp.int32, (Y, Z), 1)
     row = lax.broadcasted_iota(jnp.int32, (Y, Z), 0)
@@ -120,6 +130,9 @@
     def flat_rows(s):
         return pl.ds(0 if s == 1 else 4, X)
 
+    def line_row(k, s):
+        return (8 - DEEP if s == 1 else 0) + k % DEEP
+
     def zat(px, s):
         return (px + DEEP) * block + (DEEP - 1 if s == 1 else HALF + DEEP)
 
@@ -138,53 +151,51 @@
             acc = jnp.where(lane == at, roll(planes[x], at - (Z - 1 if s == 1 else 0), 1), acc)
         return acc
 
-    def copies(messages, ssem, rsem):
-        return [
+    def launch(messages, ssem, rsem):
+        for src, dst, off in messages:
             pltpu.make_async_remote_copy(
                 src_ref=src,
                 dst_ref=dst,
-                send_sem=ssem.at[k],
-                recv_sem=rsem.at[k],
-                device_id=device(off),
+                send_sem=ssem,
+                recv_sem=rsem,
+                device_id=place_of[off],
                 device_id_type=MESH,
-            )
-            for k, (src, dst, off) in enumerate(messages)
-        ]
-
-    def launch(flying):
-        for copy in flying:
-            copy.start()
-
-    def finish(flying):
-        for copy in flying:
-            copy.wait_recv()
-        for copy in flying:
-            copy.wait_send()
+            ).start()
+
+    def finish(messages, ssem, rsem):
+        lines = sum(math.prod(src.shape[:-1]) for src, _, _ in messages)
+        span = bulk.at[pl.ds(0, lines)]
+        for sem in (rsem, ssem):
+            pltpu.make_async_copy(span, span, sem).wait()
 
     def bundle(par):
         messages = []
+
+        def beside(a, b, c):
+            dst = fz.at[par, INDEX[c], TRAVEL[a]]
+            rows = {1: pl.ds(Y - DEEP, DEEP), -1: pl.ds(0, DEEP), 0: pl.ds(0, Y)}[b]
+            land = pl.ds({1: 8 - DEEP, -1: 8 + Y, 0: 8}[b], DEEP if b else Y)
+            planes = pl.ds(0, 1 if a and b else 2)
+            messages.append((sz.at[planes, rows, :], dst.at[planes, land, :], (a, b, c)))
+
         for c in zsides:
-            for b in (1, -1, 0):
-                for a in (1, -1, 0):
-                    dst = fz.at[par, INDEX[c], TRAVEL[a]]
-                    rows = {1: pl.ds(Y - DEEP, DEEP), -1: pl.ds(0, DEEP), 0: pl.ds(0, Y)}[b]
-                    land = {1: 8 - DEEP, -1: 8 + Y, 0: 8}[b]
-                    land = pl.ds(land, DEEP if b else Y)
-                    planes = pl.ds(0, 1 if a and b else 2)
-                    messages.append((sz.at[planes, rows, :], dst.at[planes, land, :], (a, b, c)))
+            for a, b in EDGES + [(0, 1), (0, -1)]:
+                beside(a, b, c)
         for a, b in EDGES:
             bi, ai, rows = INDEX[b], INDEX[a], deep_rows(b)
-            src = pl.ds(X - 1 if a == 1 else 0, 5)
+            src = pl.ds(X + 2 if a == 1 else 0, 8)
             messages.append((sy.at[bi, src, rows, :], rxy.at[par, bi, ai, :, rows, :], (a, b, 0)))
-            messages.append((sl.at[bi, ai], rl.at[par, bi, ai], (a, b, 0)))
         for s in SIGNS:
             si = INDEX[s]
-            for span, rows in ((MOMS + 5, flat_rows(s)), (X + 4, deep_rows(s))):
-                span = pl.ds(0, span)
-                messages.append((sy.at[si, span, rows, :], ry.at[par, si, span, rows, :], (0, s, 0)))
+            messages.append((sy.at[si, pl.ds(2, MOMS + 5)], ry.at[par, si], (0, s, 0)))
+        for c in zsides:
+            for a in SIGNS:
+                beside(a, 0, c)
         for s in SIGNS:
             messages.append((sx.at[INDEX[s]], rx.at[par, INDEX[s]], (s, 0, 0)))
-        return copies(messages, sa, ra.at[par])
+        for c in zsides:
+            beside(0, 0, c)
+        return messages, sa.at[0], ra.at[par]
 
     def farewell():
         messages = []
@@ -194,7 +205,7 @@
             messages.append((cz_.at[INDEX[s]], rcz.at[INDEX[s]], (0, 0, s)))
         for s in SIGNS:
             messages.append((cx_.at[INDEX[s]], rcx.at[INDEX[s]], (s, 0, 0)))
-        return copies(messages, sc, rc)
+        return messages, sc.at[0], rc.at[0]
 
     def moments(ps):
         rho = ps[0]
@@ -221,7 +232,9 @@
     keep = 1.0 - 1.0 / relax_time
     mix = 1.0 / relax_time - 1.0
 
-    def relaxed(ps, rho, u):
+    def relax(x):
+        ps = [pops[i, x] for i in range(19)]
+        rho, u = mom[0, x], [mom[1 + d, x] for d in range(3)]
         flat = (mix * rho) * (1.0 - 1.5 * (u[0] * u[0] + u[1] * u[1] + u[2] * u[2]))
         out = [keep * ps[0] + WEIGHTS[0] * flat]
         for i in range(1, 19, 2):
@@ -230,7 +243,8 @@
             odd = (3.0 * mix * WEIGHTS[i]) * rho * a
             out.append(keep * ps[i] + even + odd)
             out.append(keep * ps[i + 1] + even - odd)
-        return out
+        for i in range(19):
+            post[i, x] = out[i]
 
     def place(acc, v, slot, x):
         at = slot * width + x * block
@@ -241,12 +255,9 @@
         first = jnp.zeros((Y, Z), jnp.float32)
         second = jnp.zeros((Y, Z), jnp.float32)
         for x in range(X):
-            rho = mom[0, x]
-            u = [mom[1 + d, x] for d in range(3)]
-            out = relaxed([pops[i, x] for i in range(19)], rho, u)
-            heads, b = [rho] + u, base[x]
-            for i in range(19):
-                post[i, x] = out[i]
+            heads, b = [mom[g, x] for g in range(MOMS)], base[x]
+            u = heads[1:]
+            out = [pops[i, x] for i in range(19)]
             for s in SIGNS:
                 si = INDEX[s]
                 if x == xsrc(s):
@@ -261,22 +272,25 @@
                     sx[si, MOMS + 6 + DEEP, DEEP + slot : DEEP + slot + 1, :] = u[1][Y - 1 :, :]
                 y, at = ysrc(s), (0 if s == 1 else 4) + x
                 for g in range(MOMS):
-                    sy[si, g, at : at + 1, :] = heads[g][y : y + 1, :]
+                    sy[si, 2 + g, at : at + 1, :] = heads[g][y : y + 1, :]
                 for k, i in enumerate(CROSS[1][s]):
-                    sy[si, MOMS + k, at : at + 1, :] = out[i][y : y + 1, :]
+                    sy[si, 2 + MOMS + k, at : at + 1, :] = out[i][y : y + 1, :]
                 rows = slice(Y - DEEP, Y) if s == 1 else slice(0, DEEP)
-                sy[si, 2 + x, deep_rows(s), :] = b[rows, :]
+                sy[si, 5 + x, deep_rows(s), :] = b[rows, :]
                 if x == 0:
-                    sy[si, 0, deep_rows(s), :] = u[0][rows, :]
+                    sy[si, 3, deep_rows(s), :] = u[0][rows, :]
                 if x == X - 1:
-                    sy[si, X + 3, deep_rows(s), :] = u[0][rows, :]
+                    sy[si, X + 6, deep_rows(s), :] = u[0][rows, :]
                 for a in SIGNS:
+                    lines = {}
                     if x == xsrc(a):
-                        for k, v in enumerate(heads + [out[DIRS.index((a, s, 0))]]):
-                            sl[si, INDEX[a], k : k + 1, :] = v[y : y + 1, :]
+                        lines = dict(enumerate(heads + [out[DIRS.index((a, s, 0))]]))
                     slot = x - (X - DEEP) if a == 1 else x - 1
                     if 0 <= slot < DEEP - 1:
-                        sl[si, INDEX[a], 5 + slot : 6 + slot, :] = u[1][y : y + 1, :]
+                        lines[5 + slot] = u[1]
+                    for k, v in lines.items():
+                        at, sub = (X + 7 if a == 1 else 0) + k // DEEP, line_row(k, s)
+                        sy[si, at, sub : sub + 1, :] = v[y : y + 1, :]
             for g, v in enumerate([b] + heads):
                 first = place(first, v, g, x)
             for k, (up, down) in enumerate(ZPAIRS):
@@ -287,7 +301,7 @@
             si = INDEX[s]
             sx[si, MOMS + 5 + DEEP] = first
             rows = slice(Y - DEEP, Y) if s == 1 else slice(0, DEEP)
-            for at in (1, X + 2):
+            for at in (4, X + 5):
                 sy[si, at, deep_rows(s), :] = first[rows, :]
 
     def forced(rho, inv, u, force):
@@ -295,16 +309,26 @@
         flat = rho * (1.0 - 1.5 * (v[0] * v[0] + v[1] * v[1] + v[2] * v[2]))
         return v, flat
 
-    def one(i, rho, a, flat):
-        return WEIGHTS[i] * (flat + rho * (a * (3.0 + 4.5 * a)))
-
-    for ref in (sx, sy, sl, cy_, oe, oz):
+    def collide(rho, u, force):
+        v, flat = forced(rho, 1.0 / rho, u, force)
+        thin = mix * rho
+        flat = flat + thin * (1.0 - 1.5 * (u[0] * u[0] + u[1] * u[1] + u[2] * u[2]))
+
+        def hit(i, p, along_of):
+            a, b = along_of(i, u), along_of(i, v)
+            both = thin * (a * (3.0 + 4.5 * a)) + rho * (b * (3.0 + 4.5 * b))
+            return keep * p + WEIGHTS[i] * (flat + both)
+
+        return hit
+
+    for ref in (sx, sy, cy_, oe, oz):
         ref[...] = jnp.zeros_like(ref)
+    for load in loads:
+        load.wait()
 
     for x in range(X):
-        base[x] = order_in[x]
-        r = dens_in[x]
-        u = [vel_in[d, x] for d in range(3)]
+        r = dens[x]
+        u = [vel[d, x] for d in range(3)]
         usq = 1.0 - 1.5 * (u[0] * u[0] + u[1] * u[1] + u[2] * u[2])
         ps = []
         for i in range(19):
@@ -321,20 +345,22 @@
             mom[1 + d, x] = moms[d] * inv
     ready()
     pl.semaphore_wait(barrier, len(partners))
-    launch(bundle(0))
+    launch(*bundle(0))
+    for x in range(X):
+        relax(x)
 
     outer_first = sorted(range(X), key=lambda x: (min(x, X - 1 - x), x))
 
     def step(n, carry):
         par = lax.rem(n, 2)
-        finish(bundle(par))
+        finish(*bundle(par))
         low, high = ry.at[par, 0], ry.at[par, 1]
 
         def tall(a):
             if a == 0:
-                near = [low[1], sz[0], high[1]]
+                near = [low[2], sz[0], high[2]]
             else:
-                at = DEEP if a == 1 else 1
+                at = DEEP if a == 1 else DEEP + 1
                 mid = rx[par, INDEX[a], MOMS + 5 + DEEP]
                 near = [rxy[par, 0, INDEX[a], at], mid, rxy[par, 1, INDEX[a], at]]
             near = jnp.concatenate(near, axis=0)
@@ -377,28 +403,29 @@
             if px < 0:
                 return rxy[par, INDEX[s], 0, px + DEEP]
             if px >= X:
-                return rxy[par, INDEX[s], 1, 2 + px - X]
-            return ry[par, INDEX[s], 2 + px]
+                return rxy[par, INDEX[s], 1, DEEP + 2 + px - X]
+            return ry[par, INDEX[s], 3 + px]
 
         def speed(px):
             if px < 0:
                 tiles, mid = [rxy[par, k, 0, 4] for k in range(2)], rx[par, 0, 1]
             elif px >= X:
-                tiles, mid = [rxy[par, k, 1, 0] for k in range(2)], rx[par, 1, 1]
+                tiles, mid = [rxy[par, k, 1, DEEP] for k in range(2)], rx[par, 1, 1]
             else:
-                tiles, mid = [ry[par, k, 0 if px == 0 else X + 3] for k in range(2)], mom[1, px]
+                tiles, mid = [ry[par, k, 1 if px == 0 else X + 4] for k in range(2)], mom[1, px]
             return jnp.concatenate([tiles[0], mid, tiles[1]], axis=0)
 
+        def line(k, a, s):
+            at, sub = (DEEP + 2 if a == 1 else 0) + k // DEEP, line_row(k, s)
+            return rxy[par, INDEX[s], INDEX[a], at, sub : sub + 1, :]
+
         def outside(px, s):
-            si = INDEX[s]
             if px < 0:
-                at = 2 if px == -1 else 5 + px + DEEP
-                return rl[par, si, 0, at : at + 1, :]
+                return line(2 if px == -1 else 5 + px + DEEP, 1, s)
             if px >= X:
-                at = 2 if px == X else 5 + px - X - 1
-                return rl[par, si, 1, at : at + 1, :]
+                return line(2 if px == X else 5 + px - X - 1, -1, s)
             at = (0 if s == 1 else 4) + px
-            return ry[par, si, 2, at : at + 1, :]
+            return ry[par, INDEX[s], 2, at : at + 1, :]
 
         def inside(px, s):
             if 0 <= px < X:
@@ -472,33 +499,37 @@
         ]
 
         XH, YH, LH, ZH = {}, {}, {}, {}
+        own = lambda i, w: along(i, w)
         for s in SIGNS:
             si = INDEX[s]
             rho = rx[par, si, 0]
             u = [rx[par, si, 1 + d] for d in range(3)]
             px = -1 if s == 1 else X
-            v, flat = forced(rho, 1.0 / rho, u, [f[own_rows, :] for f in F[px]])
+            hit = collide(rho, u, [f[own_rows, :] for f in F[px]])
             for k, i in enumerate(CROSS[0][s]):
-                XH[i] = rx[par, si, MOMS + k] + one(i, rho, along(i, v), flat)
+                XH[i] = hit(i, rx[par, si, MOMS + k], own)
             rho = ry[par, si, 0]
             u = [ry[par, si, 1 + d] for d in range(3)]
-            v, flat = forced(rho, 1.0 / rho, u, [fy[si, d] for d in range(3)])
+            hit = collide(rho, u, [fy[si, d] for d in range(3)])
             for k, i in enumerate(CROSS[1][s]):
-                YH[i] = ry[par, si, MOMS + k] + one(i, rho, along(i, v), flat)
+                YH[i] = hit(i, ry[par, si, MOMS + k], own)
             for a in SIGNS:
                 i = DIRS.index((a, s, 0))
-                head = [rl[par, si, INDEX[a], k : k + 1, :] for k in range(5)]
+                head = [line(k, a, s) for k in range(5)]
                 y, px = (7 if s == 1 else 8 + Y), (-1 if a == 1 else X)
-                force = [f[y : y + 1, :] for f in F[px]]
-                v, flat = forced(head[0], 1.0 / head[0], head[1:4], force)
-                LH[i] = head[4] + one(i, head[0], along(i, v), flat)
-        v, flat = forced(rho_z, 1.0 / rho_z, u_z, FZ)
+                hit = collide(head[0], head[1:4], [f[y : y + 1, :] for f in F[px]])
+                LH[i] = hit(i, head[4], own)
+
+        def sided(i, w):
+            a = zsign * w[2]
+            for d in range(2):
+                if DIRS[i][d]:
+                    a = a + w[d] if DIRS[i][d] == 1 else a - w[d]
+            return a
+
+        hit = collide(rho_z, u_z, FZ)
         for k, (up, down) in enumerate(ZPAIRS):
-            a = zsign * v[2]
-            for d in range(2):
-                if DIRS[up][d]:
-                    a = a + v[d] if DIRS[up][d] == 1 else a - v[d]
-            h = packed_far(k) + one(up, rho_z, a, flat)
+            h = hit(up, packed_far(k), sided)
             ZH[up] = ZH[down] = roll(h, DIRS[up][1], 0)[own_rows, :]
 
         for x in range(X):
@@ -542,7 +573,7 @@
                 for x in range(X):
                     cy_[INDEX[s], 1 + x : 2 + x, :] = mom[2, x, y : y + 1, :]
                 cz_[INDEX[s]] = pack([mom[3, x] for x in range(X)], s)
-            launch(farewell())
+            launch(*farewell())
 
         tx = {0: 0.0, X: 0.0}
         for x in range(1, X):
@@ -557,12 +588,14 @@
         @pl.when(n < ITERS - 1)
         def _():
             ready()
-            launch(bundle(1 - par))
+            launch(*bundle(1 - par))
+            for x in range(X):
+                relax(x)
 
         return carry
 
     lax.fori_loop(0, ITERS, step, 0)
-    finish(farewell())
+    finish(*farewell())
 
     OZ = oz[own_rows, :]
     for x in range(X):
@@ -591,23 +624,24 @@
     X, Y, Z = order_param.shape
     f32 = jnp.float32
     plane, rows, tall = (Y, Z), (8, Z), (Y + 16, Z)
-    planes, tiles = MOMS + 5 + DEEP + 2, max(MOMS + 5, X + 4)
+    planes = MOMS + 5 + DEEP + 2
+    lines = 2 * planes * Y + 2 * 8 * (MOMS + 5) + 4 * 8 * DEEP
+    lines += (1 if sizes[2] == 2 else 2) * (6 * Y + 8 * DEEP)
     vmem = [
         (19, X, Y, Z), (MOMS, X, Y, Z), (X, Y, Z), (X + 2 * DEEP,) + tall, tall,
+        (X, Y, Z), (3, X, Y, Z), (lines, Z),
         (2, planes) + plane, (2, 2, planes) + plane,
-        (2, tiles) + rows, (2, 2, tiles) + rows, (2, 2, 2, 5) + rows,
-        (2, 2) + rows, (2, 2, 2) + rows,
+        (2, X + 10) + rows, (2, 2, MOMS + 5) + rows, (2, 2, 2, 8) + rows,
         (2,) + plane, (2, 2, 3, 2) + tall, (2, 3) + rows,
         (2,) + plane, (2,) + rows, (2,) + plane,
         (2,) + plane, (2,) + rows, (2,) + plane,
     ]
-    count = (9 if sizes[2] == 2 else 18) + 14
-    sems = [(count,), (2, count), (6,), (6,)]
+    sems = [(3,), (1,), (2,), (1,), (1,)]
     spec = pl.BlockSpec(memory_space=pltpu.VMEM)
     return pl.pallas_call(
         functools.partial(kernel, sizes),
         out_shape=(pltpu.VMEM((X, Y, Z), f32), pltpu.VMEM((19, X, Y, Z), f32)),
-        in_specs=[spec] * 3,
+        in_specs=[pl.BlockSpec(memory_space=pl.ANY)] * 3,
         out_specs=(spec, spec),
         scratch_shapes=[pltpu.VMEM(s, f32) for s in vmem]
         + [pltpu.SemaphoreType.DMA(n) for n in sems],

time: 49.5 us -> 47.8 us (0.966)
  Pallas kernels: 47.3 us -> 45.6 us
    pallas_call x1, Pallas kernels: 47.3 us -> 45.6 us  [on_device(): pl.pallas_call(functools.partial(kernel, sizes), out_shape=(pltpu.VMEM((X...]
where the time goes in v4:
time: 47.8 us; the launch traced here: 47.7 us
  Pallas kernels  45.6 us (95%)
  local copies, waits for them, and re-layouts  1.44 us (3%)
  between operations  0.64 us (1%)
    pallas_call x1, Pallas kernels, on_device(): pl.pallas_call(functools.partial(kernel, sizes), out_shape=(pltpu.VMEM((X...  45.6 us
    unnamed x2, local copies, waits for them, and re-layouts  1.44 us

profile of v4, /device:TPU:0, one launch (start us, length us, event | category | flops | bytes accessed | tf_op | source)
XLA Modules:
  0.0 47.7 jit_solution(12284299339530167828)
XLA Ops:
  0.6 45.6 %shard_map.50 = (f32[4,16,128]{2,1,0:T(8,128)S(1)}, f32[19,4,16,128]{3,2,1,0:T(8,128)S(1)}) custom-call(f32[4,16,128]{2,1,0:T(8,128)} %order_in.1, f32[4,16,128]{2,1,0:T(8,128)} %dens_in.1, f32[3,4,16,128]{3,2,1,0:T(8,128)} %vel_in.1), custom_call_target="tpu_custom_call" | custom-call | tf_op jit(solution)/shard_map/pallas_call | solution.py:641
  46.2 0.6 %copy.7 = f32[4,16,128]{2,1,0:T(8,128)} copy(f32[4,16,128]{2,1,0:T(8,128)S(1)} %get-tuple-element.2) | data formatting | bytes 65536
  46.8 0.8 %copy.8 = f32[19,4,16,128]{3,2,1,0:T(8,128)} copy(f32[19,4,16,128]{3,2,1,0:T(8,128)S(1)} %get-tuple-element.3) | data formatting | bytes 1245184

commit v5 on v4

--- a/solution.py
+++ b/solution.py
@@ -105,8 +105,9 @@
     face_z = column == DEEP
     face_x = (frame // block == DEEP) | (frame // block == DEEP + X)
     face_y = (erow == 8) | (erow == 8 + Y)
-    below = jnp.where(erow == 8, 1.0, jnp.where(erow == 7, -1.0, 0.0))
-    above = jnp.where(erow == 8 + Y, 1.0, jnp.where(erow == 7 + Y, -1.0, 0.0))
+    hrow = lax.broadcasted_iota(jnp.int32, (16, Z), 0)
+    seam = jnp.where(hrow == 8, 1.0, jnp.where(hrow == 7, -1.0, 0.0))
+    last = column == DEEP - 1
 
     def roll(v, s, axis):
         s = s % v.shape[axis]
@@ -133,12 +134,14 @@
     def line_row(k, s):
         return (8 - DEEP if s == 1 else 0) + k % DEEP
 
-    def zat(px, s):
-        return (px + DEEP) * block + (DEEP - 1 if s == 1 else HALF + DEEP)
-
-    def zshift(v, s, packed, at):
+    def halo_pair(v):
+        return jnp.where(last, v, roll(v, -(HALF + 2), 1))
+
+    def pick(pair, px):
+        return roll(pair, -((px + DEEP) * block + DEEP - 1), 1)
+
+    def zshift(v, s, col):
         lanes = lane if v.shape[0] == Y else elane
-        col = roll(packed, zend(s) - at, 1)
         return jnp.where(lanes == zend(s), col, roll(v, s, 1))
 
     def yshift(v, s, halo):
@@ -260,16 +263,6 @@
             out = [pops[i, x] for i in range(19)]
             for s in SIGNS:
                 si = INDEX[s]
-                if x == xsrc(s):
-                    for g in range(MOMS):
-                        sx[si, g] = heads[g]
-                    for k, i in enumerate(CROSS[0][s]):
-                        sx[si, MOMS + k] = out[i]
-                slot = x - (X - DEEP) if s == 1 else x
-                if 0 <= slot < DEEP:
-                    sx[si, MOMS + 5 + slot] = b
-                    sx[si, MOMS + 6 + DEEP, slot : slot + 1, :] = u[1][0:1, :]
-                    sx[si, MOMS + 6 + DEEP, DEEP + slot : DEEP + slot + 1, :] = u[1][Y - 1 :, :]
                 y, at = ysrc(s), (0 if s == 1 else 4) + x
                 for g in range(MOMS):
                     sy[si, 2 + g, at : at + 1, :] = heads[g][y : y + 1, :]
@@ -299,10 +292,32 @@
         sz[1] = second
         for s in SIGNS:
             si = INDEX[s]
-            sx[si, MOMS + 5 + DEEP] = first
             rows = slice(Y - DEEP, Y) if s == 1 else slice(0, DEEP)
             for at in (4, X + 5):
                 sy[si, at, deep_rows(s), :] = first[rows, :]
+
+    def ready_planes():
+        for s in SIGNS:
+            si, edge = INDEX[s], xsrc(s)
+            for g in range(MOMS):
+                sx[si, g] = mom[g, edge]
+            for k, i in enumerate(CROSS[0][s]):
+                sx[si, MOMS + k] = pops[i, edge]
+            for slot in range(DEEP):
+                x = slot + (X - DEEP if s == 1 else 0)
+                sx[si, MOMS + 5 + slot] = base[x]
+                sx[si, MOMS + 6 + DEEP, slot : slot + 1, :] = mom[2, x, 0:1, :]
+                sx[si, MOMS + 6 + DEEP, DEEP + slot : DEEP + slot + 1, :] = mom[2, x, Y - 1 :, :]
+            sx[si, MOMS + 5 + DEEP] = sz[0]
+
+    def send(par):
+        messages, ssem, rsem = bundle(par)
+        first = [m for m in messages if m[2][1]]
+        launch(first, ssem, rsem)
+        ready_planes()
+        launch(messages[len(first) :], ssem, rsem)
+        for x in range(X):
+            relax(x)
 
     def forced(rho, inv, u, force):
         v = [u[d] + force[d] * inv for d in range(3)]
@@ -345,11 +360,7 @@
             mom[1 + d, x] = moms[d] * inv
     ready()
     pl.semaphore_wait(barrier, len(partners))
-    launch(*bundle(0))
-    for x in range(X):
-        relax(x)
-
-    outer_first = sorted(range(X), key=lambda x: (min(x, X - 1 - x), x))
+    send(0)
 
     def step(n, carry):
         par = lax.rem(n, 2)
@@ -439,8 +450,34 @@
         for lo, hi in ((-1, 0), (X - 1, X)):
             t = 0.25 * (speed(lo) + speed(hi)) * (oe[lo + DEEP] + oe[hi + DEEP])
             across[lo], across[hi] = -t, t
-        OE = {}
-        for px in range(-DEEP, X + DEEP):
+        beside = roll(OZ, 1, 0) + roll(OZ, -1, 0) + roll(OZ, 1, 1) + roll(OZ, -1, 1)
+        beside = beside + roll(OZ, block, 1) + roll(OZ, -block, 1)
+        CZ = chemical(OZ, beside)
+        scale = -0.5 * OZ
+        FZ = [
+            scale * (roll(CZ, -block, 1) - roll(CZ, block, 1)),
+            scale * (roll(CZ, -1, 0) - roll(CZ, 1, 0)),
+            scale * (roll(CZ, -1, 1) - roll(CZ, 1, 1)),
+        ]
+
+        def sided(i, w):
+            a = zsign * w[2]
+            for d in range(2):
+                if DIRS[i][d]:
+                    a = a + w[d] if DIRS[i][d] == 1 else a - w[d]
+            return a
+
+        ZH = []
+        hit = collide(rho_z, u_z, FZ)
+        for k, (up, down) in enumerate(ZPAIRS):
+            h = halo_pair(hit(up, packed_far(k), sided))
+            ZH.append(roll(h, DIRS[up][1], 0)[own_rows, :])
+        own_pair = jnp.where(column == DEEP, OZ, roll(OZ, -HALF, 1))
+        order_pair, chem_pair = halo_pair(OZ), halo_pair(CZ)
+
+        OE, C, F = {}, {}, {}
+
+        def complete(px):
             if px < 0:
                 mid = rx[par, 0, MOMS + 5 + px + DEEP]
             elif px >= X:
@@ -450,33 +487,29 @@
             v = jnp.concatenate([around(px, 1), mid, around(px, -1)], axis=0)
             if px in across:
                 v = v + across[px]
-            for s, sign, y in ((1, below, 8), (-1, above, 8 + Y)):
+            parts = []
+            for s, sign, y in ((1, 1.0, 8), (-1, -1.0, 8 + Y)):
                 pair = oe[px + DEEP, y - 1 : y, :] + oe[px + DEEP, y : y + 1, :]
                 t = 0.25 * (outside(px, s) + inside(px, s)) * pair
-                v = v + sign * jnp.broadcast_to(t, v.shape)
-            at = (px + DEEP) * block
-            v = jnp.where(elane == 0, roll(OZ, -(at + DEEP), 1), v)
-            v = jnp.where(elane == Z - 1, roll(OZ, Z - 1 - (HALF + at + DEEP - 1), 1), v)
-            OE[px] = v
-        for px in range(-DEEP, X + DEEP):
-            oe[px + DEEP] = OE[px]
-        O = [OE[x][own_rows, :] for x in range(X)]
-
-        C = {}
-        for px in range(-2, X + 2):
-            o = OE[px]
+                parts.append(seam * jnp.broadcast_to(t, (16, Z)))
+            half = E // 2
+            if half == 16:
+                v = v + jnp.concatenate(parts, axis=0)
+            else:
+                gap = jnp.zeros((E - 32, Z), jnp.float32)
+                v = v + jnp.concatenate([parts[0], gap, parts[1]], axis=0)
+            col = roll(own_pair, -((px + DEEP) * block + DEEP), 1)
+            OE[px] = jnp.where((elane == 0) | (elane == Z - 1), col, v)
+
+        def potential(px):
+            o, col = OE[px], pick(order_pair, px)
             beside = OE[px - 1] + OE[px + 1] + roll(o, 1, 0) + roll(o, -1, 0)
-            beside = beside + zshift(o, 1, OZ, zat(px, 1)) + zshift(o, -1, OZ, zat(px, -1))
-            C[px] = chemical(o, beside)
-        beside = roll(OZ, 1, 0) + roll(OZ, -1, 0) + roll(OZ, 1, 1) + roll(OZ, -1, 1)
-        beside = beside + roll(OZ, block, 1) + roll(OZ, -block, 1)
-        CZ = chemical(OZ, beside)
-
-        F = {}
-        for px in range(-1, X + 1):
-            c = C[px]
+            C[px] = chemical(o, beside + zshift(o, 1, col) + zshift(o, -1, col))
+
+        def push(px):
+            c, col = C[px], pick(chem_pair, px)
             y_dn, y_up = roll(c, 1, 0), roll(c, -1, 0)
-            z_dn, z_up = zshift(c, 1, CZ, zat(px, 1)), zshift(c, -1, CZ, zat(px, -1))
+            z_dn, z_up = zshift(c, 1, col), zshift(c, -1, col)
             scale = -0.5 * OE[px]
             F[px] = [
                 scale * (C[px + 1] - C[px - 1]),
@@ -485,67 +518,64 @@
             ]
             if 0 <= px < X:
                 lap = C[px + 1] + C[px - 1] + y_up + y_dn + z_up + z_dn - 6.0 * c
-                base[px] = O[px] + mobility * lap[own_rows, :]
+                base[px] = (OE[px] + mobility * lap)[own_rows, :]
                 for s in SIGNS:
                     at = (0 if s == 1 else 4) + px
                     y = 7 if s == 1 else 8 + Y
                     for d in range(3):
                         fy[INDEX[s], d, at : at + 1, :] = F[px][d][y : y + 1, :]
-        scale = -0.5 * OZ
-        FZ = [
-            scale * (roll(CZ, -block, 1) - roll(CZ, block, 1)),
-            scale * (roll(CZ, -1, 0) - roll(CZ, 1, 0)),
-            scale * (roll(CZ, -1, 1) - roll(CZ, 1, 1)),
-        ]
-
-        XH, YH, LH, ZH = {}, {}, {}, {}
-        own = lambda i, w: along(i, w)
+
+        XH, YH, LH = {}, {}, {}
+
+        def strike(px):
+            if 0 <= px < X:
+                rho = mom[0, px]
+                u = [mom[1 + d, px] for d in range(3)]
+                v, flat = forced(rho, 1.0 / rho, u, [f[own_rows, :] for f in F[px]])
+                post[0, px] = post[0, px] + WEIGHTS[0] * flat
+                for i in range(1, 19, 2):
+                    a = along(i, v)
+                    even = WEIGHTS[i] * flat + (4.5 * WEIGHTS[i]) * rho * (a * a)
+                    odd = (3.0 * WEIGHTS[i]) * rho * a
+                    post[i, px] = post[i, px] + even + odd
+                    post[i + 1, px] = post[i + 1, px] + even - odd
+                return
+            a = 1 if px < 0 else -1
+            ai = INDEX[a]
+            rho = rx[par, ai, 0]
+            u = [rx[par, ai, 1 + d] for d in range(3)]
+            hit = collide(rho, u, [f[own_rows, :] for f in F[px]])
+            for k, i in enumerate(CROSS[0][a]):
+                XH[i] = hit(i, rx[par, ai, MOMS + k], along)
+            for s in SIGNS:
+                i = DIRS.index((a, s, 0))
+                head = [line(k, a, s) for k in range(5)]
+                y = 7 if s == 1 else 8 + Y
+                hit = collide(head[0], head[1:4], [f[y : y + 1, :] for f in F[px]])
+                LH[i] = hit(i, head[4], along)
+
+        for px in range(-DEEP, X + DEEP):
+            complete(px)
+            if px - 1 >= -2:
+                potential(px - 1)
+            if px - 2 >= -1:
+                push(px - 2)
+                strike(px - 2)
+        for px in range(-DEEP, X + DEEP):
+            oe[px + DEEP] = OE[px]
+        O = [OE[x][own_rows, :] for x in range(X)]
         for s in SIGNS:
             si = INDEX[s]
-            rho = rx[par, si, 0]
-            u = [rx[par, si, 1 + d] for d in range(3)]
-            px = -1 if s == 1 else X
-            hit = collide(rho, u, [f[own_rows, :] for f in F[px]])
-            for k, i in enumerate(CROSS[0][s]):
-                XH[i] = hit(i, rx[par, si, MOMS + k], own)
             rho = ry[par, si, 0]
             u = [ry[par, si, 1 + d] for d in range(3)]
             hit = collide(rho, u, [fy[si, d] for d in range(3)])
             for k, i in enumerate(CROSS[1][s]):
-                YH[i] = hit(i, ry[par, si, MOMS + k], own)
-            for a in SIGNS:
-                i = DIRS.index((a, s, 0))
-                head = [line(k, a, s) for k in range(5)]
-                y, px = (7 if s == 1 else 8 + Y), (-1 if a == 1 else X)
-                hit = collide(head[0], head[1:4], [f[y : y + 1, :] for f in F[px]])
-                LH[i] = hit(i, head[4], own)
-
-        def sided(i, w):
-            a = zsign * w[2]
-            for d in range(2):
-                if DIRS[i][d]:
-                    a = a + w[d] if DIRS[i][d] == 1 else a - w[d]
-            return a
-
-        hit = collide(rho_z, u_z, FZ)
-        for k, (up, down) in enumerate(ZPAIRS):
-            h = hit(up, packed_far(k), sided)
-            ZH[up] = ZH[down] = roll(h, DIRS[up][1], 0)[own_rows, :]
-
+                YH[i] = hit(i, ry[par, si, MOMS + k], along)
+
+        flows = {}
+        pair_of = {i: k for k, both in enumerate(ZPAIRS) for i in both}
         for x in range(X):
-            rho = mom[0, x]
-            u = [mom[1 + d, x] for d in range(3)]
-            v, flat = forced(rho, 1.0 / rho, u, [f[own_rows, :] for f in F[x]])
-            post[0, x] = post[0, x] + WEIGHTS[0] * flat
-            for i in range(1, 19, 2):
-                a = along(i, v)
-                even = WEIGHTS[i] * flat + (4.5 * WEIGHTS[i]) * rho * (a * a)
-                odd = (3.0 * WEIGHTS[i]) * rho * a
-                post[i, x] = post[i, x] + even + odd
-                post[i + 1, x] = post[i + 1, x] + even - odd
-
-        flows = {}
-        for x in outer_first:
+            cols = [pick(ZH[k], x - DIRS[up][0]) for k, (up, _) in enumerate(ZPAIRS)]
             ps = []
             for i, (cx, cy, cz) in enumerate(DIRS):
                 xs = x - cx
@@ -555,7 +585,7 @@
                     at = (0 if cy == 1 else 4) + xs
                     p = yshift(p, cy, YH[i][at : at + 1, :] if own else LH[i])
                 if cz:
-                    p = zshift(p, cz, ZH[i], zat(xs, cz))
+                    p = zshift(p, cz, cols[pair_of[i]])
                 pops[i, x] = p
                 ps.append(p)
             rho, moms = moments(ps)
@@ -588,16 +618,14 @@
         @pl.when(n < ITERS - 1)
         def _():
             ready()
-            launch(*bundle(1 - par))
-            for x in range(X):
-                relax(x)
+            send(1 - par)
 
         return carry
 
     lax.fori_loop(0, ITERS, step, 0)
     finish(*farewell())
 
-    OZ = oz[own_rows, :]
+    pair = halo_pair(oz[...])[own_rows, :]
     for x in range(X):
         o, u = oe[x + DEEP, own_rows, :], [mom[1 + d, x] for d in range(3)]
         change = jnp.zeros((Y, Z), jnp.float32)
@@ -613,7 +641,7 @@
                 oe[x + DEEP, at : at + 1, :] + oe[x + DEEP, 8 + y : 9 + y, :]
             )
             t = jnp.where(row == y, jnp.broadcast_to(t, (Y, Z)), 0.0)
-            side = roll(OZ, zend(s) - zat(x, s), 1)
+            side = pick(pair, x)
             beside = roll(rcz[INDEX[s]], zend(s) - (1 + x), 1)
             t = t + jnp.where(lane == zend(s), (u[2] + beside) * (o + side), 0.0)
             change = change + t if s == 1 else change - t

time: 47.8 us -> 46.3 us (0.969)
  Pallas kernels: 45.6 us -> 44.1 us
    pallas_call x1, Pallas kernels: 45.6 us -> 44.1 us  [on_device(): pl.pallas_call(functools.partial(kernel, sizes), out_shape=(pltpu.VMEM((X...]
where the time goes in v5:
time: 46.3 us; the launch traced here: 46.1 us
  Pallas kernels  44.1 us (95%)
  local copies, waits for them, and re-layouts  1.44 us (3%)
  between operations  0.64 us (1%)
    pallas_call x1, Pallas kernels, on_device(): pl.pallas_call(functools.partial(kernel, sizes), out_shape=(pltpu.VMEM((X...  44.1 us
    unnamed x2, local copies, waits for them, and re-layouts  1.44 us

profile of v5, /device:TPU:0, one launch (start us, length us, event | category | flops | bytes accessed | tf_op | source)
XLA Modules:
  0.0 46.1 jit_solution(16045358672067863318)
XLA Ops:
  0.6 44.1 %shard_map.50 = (f32[4,16,128]{2,1,0:T(8,128)S(1)}, f32[19,4,16,128]{3,2,1,0:T(8,128)S(1)}) custom-call(f32[4,16,128]{2,1,0:T(8,128)} %order_in.1, f32[4,16,128]{2,1,0:T(8,128)} %dens_in.1, f32[3,4,16,128]{3,2,1,0:T(8,128)} %vel_in.1), custom_call_target="tpu_custom_call" | custom-call | tf_op jit(solution)/shard_map/pallas_call | solution.py:669
  44.7 0.6 %copy.7 = f32[4,16,128]{2,1,0:T(8,128)} copy(f32[4,16,128]{2,1,0:T(8,128)S(1)} %get-tuple-element.2) | data formatting | bytes 65536
  45.3 0.8 %copy.8 = f32[19,4,16,128]{3,2,1,0:T(8,128)} copy(f32[19,4,16,128]{3,2,1,0:T(8,128)S(1)} %get-tuple-element.3) | data formatting | bytes 1245184

commit v6 on v5

--- a/solution.py
+++ b/solution.py
@@ -59,8 +59,8 @@
     (cx_, cy_, cz_, rcx, rcy, rcz) = scratch[16:22]
     (si_, sa, ra, sc, rc) = scratch[22:27]
     X, Y, Z = order.shape
-    E = Y + 16
-    own_rows = slice(8, 8 + Y)
+    E = Y + 8
+    own_rows = slice(0, Y)
     block = 2 * DEEP
     width = X * block
     me = [lax.axis_index(a) for a in AXES]
@@ -104,10 +104,12 @@
     low_col = lane < HALF
     face_z = column == DEEP
     face_x = (frame // block == DEEP) | (frame // block == DEEP + X)
-    face_y = (erow == 8) | (erow == 8 + Y)
-    hrow = lax.broadcasted_iota(jnp.int32, (16, Z), 0)
-    seam = jnp.where(hrow == 8, 1.0, jnp.where(hrow == 7, -1.0, 0.0))
+    face_y = (erow == 0) | (erow == Y)
+    sub = lax.broadcasted_iota(jnp.int32, (8, Z), 0)
     last = column == DEEP - 1
+
+    def extend(mid, low, high):
+        return jnp.concatenate([mid, jnp.where(sub < 4, high, low)], axis=0)
 
     def roll(v, s, axis):
         s = s % v.shape[axis]
@@ -124,6 +126,9 @@
 
     def ysrc(s):
         return Y - 1 if s == 1 else 0
+
+    def next_row(s):
+        return E - 1 if s == 1 else Y
 
     def deep_rows(s):
         return pl.ds(8 - DEEP if s == 1 else 0, DEEP)
@@ -177,7 +182,7 @@
         def beside(a, b, c):
             dst = fz.at[par, INDEX[c], TRAVEL[a]]
             rows = {1: pl.ds(Y - DEEP, DEEP), -1: pl.ds(0, DEEP), 0: pl.ds(0, Y)}[b]
-            land = pl.ds({1: 8 - DEEP, -1: 8 + Y, 0: 8}[b], DEEP if b else Y)
+            land = pl.ds({1: E - DEEP, -1: Y, 0: 0}[b], DEEP if b else Y)
             planes = pl.ds(0, 1 if a and b else 2)
             messages.append((sz.at[planes, rows, :], dst.at[planes, land, :], (a, b, c)))
 
@@ -211,15 +216,12 @@
         return messages, sc.at[0], rc.at[0]
 
     def moments(ps):
-        rho = ps[0]
-        for i in range(1, 19):
-            rho = rho + ps[i]
-        moms = []
-        for d in range(3):
-            up = functools.reduce(lambda a, b: a + b, [ps[i] for i in CROSS[d][1]])
-            down = functools.reduce(lambda a, b: a + b, [ps[i] for i in CROSS[d][-1]])
-            moms.append(up - down)
-        return rho, moms
+        def total(which):
+            return functools.reduce(lambda a, b: a + b, [ps[i] for i in which])
+
+        sums = [[total(CROSS[d][s]) for s in SIGNS] for d in range(3)]
+        still = total([i for i in range(19) if DIRS[i][0] == 0])
+        return still + sums[0][0] + sums[0][1], [up - down for up, down in sums]
 
     def chemical(o, beside):
         return quadratic * o + quartic * o * o * o - stiffness * (beside - 6.0 * o)
@@ -369,12 +371,11 @@
 
         def tall(a):
             if a == 0:
-                near = [low[2], sz[0], high[2]]
+                near = extend(sz[0], low[2], high[2])
             else:
                 at = DEEP if a == 1 else DEEP + 1
                 mid = rx[par, INDEX[a], MOMS + 5 + DEEP]
-                near = [rxy[par, 0, INDEX[a], at], mid, rxy[par, 1, INDEX[a], at]]
-            near = jnp.concatenate(near, axis=0)
+                near = extend(mid, rxy[par, 0, INDEX[a], at], rxy[par, 1, INDEX[a], at])
             far = [fz[par, INDEX[c], TRAVEL[a], 0] for c in zsides]
             halves = [jnp.where(facing, far[0], near), jnp.where(facing, near, far[-1])]
             return [roll(v, -a * width, 1) for v in halves]
@@ -424,7 +425,7 @@
                 tiles, mid = [rxy[par, k, 1, DEEP] for k in range(2)], rx[par, 1, 1]
             else:
                 tiles, mid = [ry[par, k, 1 if px == 0 else X + 4] for k in range(2)], mom[1, px]
-            return jnp.concatenate([tiles[0], mid, tiles[1]], axis=0)
+            return extend(mid, tiles[0], tiles[1])
 
         def line(k, a, s):
             at, sub = (DEEP + 2 if a == 1 else 0) + k // DEEP, line_row(k, s)
@@ -484,20 +485,20 @@
                 mid = rx[par, 1, MOMS + 5 + px - X]
             else:
                 mid = base[px]
-            v = jnp.concatenate([around(px, 1), mid, around(px, -1)], axis=0)
+            v = extend(mid, around(px, 1), around(px, -1))
             if px in across:
                 v = v + across[px]
-            parts = []
-            for s, sign, y in ((1, 1.0, 8), (-1, -1.0, 8 + Y)):
-                pair = oe[px + DEEP, y - 1 : y, :] + oe[px + DEEP, y : y + 1, :]
-                t = 0.25 * (outside(px, s) + inside(px, s)) * pair
-                parts.append(seam * jnp.broadcast_to(t, (16, Z)))
-            half = E // 2
-            if half == 16:
-                v = v + jnp.concatenate(parts, axis=0)
-            else:
-                gap = jnp.zeros((E - 32, Z), jnp.float32)
-                v = v + jnp.concatenate([parts[0], gap, parts[1]], axis=0)
+            t = {}
+            for s in SIGNS:
+                y, z = yend(s), next_row(s)
+                pair = oe[px + DEEP, y : y + 1, :] + oe[px + DEEP, z : z + 1, :]
+                line_t = 0.25 * (outside(px, s) + inside(px, s)) * pair
+                t[s] = jnp.broadcast_to(line_t, (8, Z))
+            halo = v[Y:, :] + jnp.where(sub == 0, t[-1], jnp.where(sub == 7, -t[1], 0.0))
+            head = v[:8, :] + jnp.where(sub == 0, t[1], 0.0)
+            tail = v[Y - 8 : Y, :] - jnp.where(sub == 7, t[-1], 0.0)
+            rest = [v[8 : Y - 8, :]] if Y > 16 else []
+            v = jnp.concatenate([head] + rest + [tail, halo], axis=0)
             col = roll(own_pair, -((px + DEEP) * block + DEEP), 1)
             OE[px] = jnp.where((elane == 0) | (elane == Z - 1), col, v)
 
@@ -521,7 +522,7 @@
                 base[px] = (OE[px] + mobility * lap)[own_rows, :]
                 for s in SIGNS:
                     at = (0 if s == 1 else 4) + px
-                    y = 7 if s == 1 else 8 + Y
+                    y = next_row(s)
                     for d in range(3):
                         fy[INDEX[s], d, at : at + 1, :] = F[px][d][y : y + 1, :]
 
@@ -550,7 +551,7 @@
             for s in SIGNS:
                 i = DIRS.index((a, s, 0))
                 head = [line(k, a, s) for k in range(5)]
-                y = 7 if s == 1 else 8 + Y
+                y = next_row(s)
                 hit = collide(head[0], head[1:4], [f[y : y + 1, :] for f in F[px]])
                 LH[i] = hit(i, head[4], along)
 
@@ -634,11 +635,11 @@
         if x == X - 1:
             change = change - (u[0] + rcx[1]) * (o + oe[DEEP + X, own_rows, :])
         for s in SIGNS:
-            at = 7 if s == 1 else 8 + Y
+            at = next_row(s)
             other = rcy[INDEX[s], 1 + x : 2 + x, :]
             y = yend(s)
             t = (mom[2, x, y : y + 1, :] + other) * (
-                oe[x + DEEP, at : at + 1, :] + oe[x + DEEP, 8 + y : 9 + y, :]
+                oe[x + DEEP, at : at + 1, :] + oe[x + DEEP, y : y + 1, :]
             )
             t = jnp.where(row == y, jnp.broadcast_to(t, (Y, Z)), 0.0)
             side = pick(pair, x)
@@ -651,7 +652,7 @@
 def on_device(sizes, order_param, density, velocity):
     X, Y, Z = order_param.shape
     f32 = jnp.float32
-    plane, rows, tall = (Y, Z), (8, Z), (Y + 16, Z)
+    plane, rows, tall = (Y, Z), (8, Z), (Y + 8, Z)
     planes = MOMS + 5 + DEEP + 2
     lines = 2 * planes * Y + 2 * 8 * (MOMS + 5) + 4 * 8 * DEEP
     lines += (1 if sizes[2] == 2 else 2) * (6 * Y + 8 * DEEP)

time: 46.3 us -> 45.9 us (level)
  no operation moved by 1% of the time
where the time goes in v6:
time: 45.9 us; the launch traced here: 45.8 us
  Pallas kernels  43.7 us (95%)
  local copies, waits for them, and re-layouts  1.44 us (3%)
  between operations  0.64 us (1%)
    pallas_call x1, Pallas kernels, on_device(): pl.pallas_call(functools.partial(kernel, sizes), out_shape=(pltpu.VMEM((X...  43.7 us
    unnamed x2, local copies, waits for them, and re-layouts  1.44 us

profile of v6, /device:TPU:0, one launch (start us, length us, event | category | flops | bytes accessed | tf_op | source)
XLA Modules:
  0.0 45.8 jit_solution(12563820777121657305)
XLA Ops:
  0.6 43.7 %shard_map.50 = (f32[4,16,128]{2,1,0:T(8,128)S(1)}, f32[19,4,16,128]{3,2,1,0:T(8,128)S(1)}) custom-call(f32[4,16,128]{2,1,0:T(8,128)} %order_in.1, f32[4,16,128]{2,1,0:T(8,128)} %dens_in.1, f32[3,4,16,128]{3,2,1,0:T(8,128)} %vel_in.1), custom_call_target="tpu_custom_call" | custom-call | tf_op jit(solution)/shard_map/pallas_call | solution.py:670
  44.3 0.6 %copy.7 = f32[4,16,128]{2,1,0:T(8,128)} copy(f32[4,16,128]{2,1,0:T(8,128)S(1)} %get-tuple-element.2) | data formatting | bytes 65536
  44.9 0.8 %copy.8 = f32[19,4,16,128]{3,2,1,0:T(8,128)} copy(f32[19,4,16,128]{3,2,1,0:T(8,128)S(1)} %get-tuple-element.3) | data formatting | bytes 1245184

commit v7 on v6

--- a/solution.py
+++ b/solution.py
@@ -55,9 +55,9 @@
 
 def kernel(sizes, order_in, dens_in, vel_in, order, pops, *scratch):
     (post, mom, base, oe, oz, dens, vel, bulk) = scratch[0:8]
-    (sx, rx, sy, ry, rxy, sz, fz, fy) = scratch[8:16]
-    (cx_, cy_, cz_, rcx, rcy, rcz) = scratch[16:22]
-    (si_, sa, ra, sc, rc) = scratch[22:27]
+    (sx, rx, sy, ry, sxy, rxy, sz, fz, fy, fp) = scratch[8:18]
+    (cx_, cy_, cz_, rcx, rcy, rcz) = scratch[18:24]
+    (si_, sa, ra, sc, rc) = scratch[24:29]
     X, Y, Z = order.shape
     E = Y + 8
     own_rows = slice(0, Y)
@@ -136,8 +136,20 @@
     def flat_rows(s):
         return pl.ds(0 if s == 1 else 4, X)
 
-    def line_row(k, s):
-        return (8 - DEEP if s == 1 else 0) + k % DEEP
+    def spare(s):
+        return 4 if s == 1 else 3
+
+    def deep_row(depth, s):
+        return 7 - depth if s == 1 else depth
+
+    def deep_tile(far, a):
+        return DEEP - far if a == 1 else far - 1
+
+    def slot_of(k, a, s):
+        free = [(2, 2), (3, 1), (3, 2)]
+        if k < 3:
+            return deep_tile(free[k][0], a), deep_row(free[k][1], s)
+        return DEEP + 2, deep_row(k - 3, s)
 
     def halo_pair(v):
         return jnp.where(last, v, roll(v, -(HALF + 2), 1))
@@ -191,11 +203,11 @@
                 beside(a, b, c)
         for a, b in EDGES:
             bi, ai, rows = INDEX[b], INDEX[a], deep_rows(b)
-            src = pl.ds(X + 2 if a == 1 else 0, 8)
-            messages.append((sy.at[bi, src, rows, :], rxy.at[par, bi, ai, :, rows, :], (a, b, 0)))
+            src, dst = sxy.at[bi, ai, :, rows, :], rxy.at[par, bi, ai, :, rows, :]
+            messages.append((src, dst, (a, b, 0)))
         for s in SIGNS:
             si = INDEX[s]
-            messages.append((sy.at[si, pl.ds(2, MOMS + 5)], ry.at[par, si], (0, s, 0)))
+            messages.append((sy.at[si], ry.at[par, si], (0, s, 0)))
         for c in zsides:
             for a in SIGNS:
                 beside(a, 0, c)
@@ -266,26 +278,33 @@
             for s in SIGNS:
                 si = INDEX[s]
                 y, at = ysrc(s), (0 if s == 1 else 4) + x
-                for g in range(MOMS):
-                    sy[si, 2 + g, at : at + 1, :] = heads[g][y : y + 1, :]
-                for k, i in enumerate(CROSS[1][s]):
-                    sy[si, 2 + MOMS + k, at : at + 1, :] = out[i][y : y + 1, :]
+                for k, v in enumerate(heads + [out[i] for i in CROSS[1][s][:-1]]):
+                    sy[si, k, at : at + 1, :] = v[y : y + 1, :]
+                v, at = out[CROSS[1][s][-1]], spare(s)
+                sy[si, x, at : at + 1, :] = v[y : y + 1, :]
                 rows = slice(Y - DEEP, Y) if s == 1 else slice(0, DEEP)
-                sy[si, 5 + x, deep_rows(s), :] = b[rows, :]
+                sy[si, 2 + x, deep_rows(s), :] = b[rows, :]
                 if x == 0:
-                    sy[si, 3, deep_rows(s), :] = u[0][rows, :]
+                    sy[si, 0, deep_rows(s), :] = u[0][rows, :]
                 if x == X - 1:
-                    sy[si, X + 6, deep_rows(s), :] = u[0][rows, :]
+                    sy[si, X + 2, deep_rows(s), :] = u[0][rows, :]
                 for a in SIGNS:
+                    ai, far = INDEX[a], X - x if a == 1 else x + 1
                     lines = {}
-                    if x == xsrc(a):
-                        lines = dict(enumerate(heads + [out[DIRS.index((a, s, 0))]]))
-                    slot = x - (X - DEEP) if a == 1 else x - 1
-                    if 0 <= slot < DEEP - 1:
-                        lines[5 + slot] = u[1]
+                    if far <= DEEP:
+                        keep_rows = DEEP + 1 - far
+                        lo = 8 - keep_rows if s == 1 else 0
+                        part = slice(Y - keep_rows, Y) if s == 1 else slice(0, keep_rows)
+                        at = deep_tile(far, a)
+                        sxy[si, ai, at, lo : lo + keep_rows, :] = b[part, :]
+                    if far == 1:
+                        sxy[si, ai, DEEP, deep_rows(s), :] = u[0][rows, :]
+                        lines = {0: heads[0], 1: u[1], 2: u[2], 3: out[DIRS.index((a, s, 0))]}
+                    elif far <= DEEP:
+                        lines = {2 + far: u[1]}
                     for k, v in lines.items():
-                        at, sub = (X + 7 if a == 1 else 0) + k // DEEP, line_row(k, s)
-                        sy[si, at, sub : sub + 1, :] = v[y : y + 1, :]
+                        at, r = slot_of(k, a, s)
+                        sxy[si, ai, at, r : r + 1, :] = v[y : y + 1, :]
             for g, v in enumerate([b] + heads):
                 first = place(first, v, g, x)
             for k, (up, down) in enumerate(ZPAIRS):
@@ -295,8 +314,9 @@
         for s in SIGNS:
             si = INDEX[s]
             rows = slice(Y - DEEP, Y) if s == 1 else slice(0, DEEP)
-            for at in (4, X + 5):
-                sy[si, at, deep_rows(s), :] = first[rows, :]
+            sy[si, 1, deep_rows(s), :] = first[rows, :]
+            for ai in range(2):
+                sxy[si, ai, DEEP + 1, deep_rows(s), :] = first[rows, :]
 
     def ready_planes():
         for s in SIGNS:
@@ -338,7 +358,7 @@
 
         return hit
 
-    for ref in (sx, sy, cy_, oe, oz):
+    for ref in (sx, sy, sxy, cy_, oe, oz):
         ref[...] = jnp.zeros_like(ref)
     for load in loads:
         load.wait()
@@ -371,10 +391,9 @@
 
         def tall(a):
             if a == 0:
-                near = extend(sz[0], low[2], high[2])
+                near = extend(sz[0], low[1], high[1])
             else:
-                at = DEEP if a == 1 else DEEP + 1
-                mid = rx[par, INDEX[a], MOMS + 5 + DEEP]
+                mid, at = rx[par, INDEX[a], MOMS + 5 + DEEP], DEEP + 1
                 near = extend(mid, rxy[par, 0, INDEX[a], at], rxy[par, 1, INDEX[a], at])
             far = [fz[par, INDEX[c], TRAVEL[a], 0] for c in zsides]
             halves = [jnp.where(facing, far[0], near), jnp.where(facing, near, far[-1])]
@@ -415,27 +434,27 @@
             if px < 0:
                 return rxy[par, INDEX[s], 0, px + DEEP]
             if px >= X:
-                return rxy[par, INDEX[s], 1, DEEP + 2 + px - X]
-            return ry[par, INDEX[s], 3 + px]
+                return rxy[par, INDEX[s], 1, px - X]
+            return ry[par, INDEX[s], 2 + px]
 
         def speed(px):
             if px < 0:
-                tiles, mid = [rxy[par, k, 0, 4] for k in range(2)], rx[par, 0, 1]
+                tiles, mid = [rxy[par, k, 0, DEEP] for k in range(2)], rx[par, 0, 1]
             elif px >= X:
                 tiles, mid = [rxy[par, k, 1, DEEP] for k in range(2)], rx[par, 1, 1]
             else:
-                tiles, mid = [ry[par, k, 1 if px == 0 else X + 4] for k in range(2)], mom[1, px]
+                tiles, mid = [ry[par, k, 0 if px == 0 else X + 2] for k in range(2)], mom[1, px]
             return extend(mid, tiles[0], tiles[1])
 
         def line(k, a, s):
-            at, sub = (DEEP + 2 if a == 1 else 0) + k // DEEP, line_row(k, s)
-            return rxy[par, INDEX[s], INDEX[a], at, sub : sub + 1, :]
+            at, r = slot_of(k, a, s)
+            return rxy[par, INDEX[s], INDEX[a], at, r : r + 1, :]
 
         def outside(px, s):
             if px < 0:
-                return line(2 if px == -1 else 5 + px + DEEP, 1, s)
+                return line(1 if px == -1 else 2 - px, 1, s)
             if px >= X:
-                return line(2 if px == X else 5 + px - X - 1, -1, s)
+                return line(1 if px == X else 3 + px - X, -1, s)
             at = (0 if s == 1 else 4) + px
             return ry[par, INDEX[s], 2, at : at + 1, :]
 
@@ -550,7 +569,9 @@
                 XH[i] = hit(i, rx[par, ai, MOMS + k], along)
             for s in SIGNS:
                 i = DIRS.index((a, s, 0))
-                head = [line(k, a, s) for k in range(5)]
+                r = deep_row(0, s)
+                side = rxy[par, INDEX[s], ai, DEEP, r : r + 1, :]
+                head = [line(0, a, s), side] + [line(k, a, s) for k in (1, 2, 3)]
                 y = next_row(s)
                 hit = collide(head[0], head[1:4], [f[y : y + 1, :] for f in F[px]])
                 LH[i] = hit(i, head[4], along)
@@ -570,8 +591,12 @@
             rho = ry[par, si, 0]
             u = [ry[par, si, 1 + d] for d in range(3)]
             hit = collide(rho, u, [fy[si, d] for d in range(3)])
+            for x in range(X):
+                at, r = (0 if s == 1 else 4) + x, spare(s)
+                fp[si, at : at + 1, :] = ry[par, si, x, r : r + 1, :]
             for k, i in enumerate(CROSS[1][s]):
-                YH[i] = hit(i, ry[par, si, MOMS + k], along)
+                p = ry[par, si, MOMS + k] if k < 4 else fp[si]
+                YH[i] = hit(i, p, along)
 
         flows = {}
         pair_of = {i: k for k, both in enumerate(ZPAIRS) for i in both}
@@ -654,20 +679,21 @@
     f32 = jnp.float32
     plane, rows, tall = (Y, Z), (8, Z), (Y + 8, Z)
     planes = MOMS + 5 + DEEP + 2
-    lines = 2 * planes * Y + 2 * 8 * (MOMS + 5) + 4 * 8 * DEEP
+    lines = 2 * planes * Y + 2 * 8 * (MOMS + 4) + 4 * (DEEP + 3) * DEEP
     lines += (1 if sizes[2] == 2 else 2) * (6 * Y + 8 * DEEP)
     vmem = [
         (19, X, Y, Z), (MOMS, X, Y, Z), (X, Y, Z), (X + 2 * DEEP,) + tall, tall,
         (X, Y, Z), (3, X, Y, Z), (lines, Z),
         (2, planes) + plane, (2, 2, planes) + plane,
-        (2, X + 10) + rows, (2, 2, MOMS + 5) + rows, (2, 2, 2, 8) + rows,
-        (2,) + plane, (2, 2, 3, 2) + tall, (2, 3) + rows,
+        (2, MOMS + 4) + rows, (2, 2, MOMS + 4) + rows,
+        (2, 2, DEEP + 3) + rows, (2, 2, 2, DEEP + 3) + rows,
+        (2,) + plane, (2, 2, 3, 2) + tall, (2, 3) + rows, (2,) + rows,
         (2,) + plane, (2,) + rows, (2,) + plane,
         (2,) + plane, (2,) + rows, (2,) + plane,
     ]
     sems = [(3,), (1,), (2,), (1,), (1,)]
     spec = pl.BlockSpec(memory_space=pltpu.VMEM)
-    return pl.pallas_call(
+    kept = pl.pallas_call(
         functools.partial(kernel, sizes),
         out_shape=(pltpu.VMEM((X, Y, Z), f32), pltpu.VMEM((19, X, Y, Z), f32)),
         in_specs=[pl.BlockSpec(memory_space=pl.ANY)] * 3,
@@ -676,6 +702,26 @@
         + [pltpu.SemaphoreType.DMA(n) for n in sems],
         compiler_params=pltpu.CompilerParams(collective_id=0, has_side_effects=True),
     )(order_param, density, velocity)
+    whole = pl.BlockSpec(memory_space=pl.ANY)
+    return pl.pallas_call(
+        write_out,
+        out_shape=tuple(jax.ShapeDtypeStruct(v.shape, f32) for v in kept),
+        in_specs=[whole] * 2,
+        out_specs=(whole, whole),
+        scratch_shapes=[pltpu.SemaphoreType.DMA((2,))],
+        compiler_params=pltpu.CompilerParams(vmem_limit_bytes=1 << 20),
+    )(*kept)
+
+
+def write_out(order, pops, order_out, pops_out, sem):
+    both = [
+        pltpu.make_async_copy(pops, pops_out, sem.at[0]),
+        pltpu.make_async_copy(order, order_out, sem.at[1]),
+    ]
+    for copy in both:
+        copy.start()
+    for copy in both:
+        copy.wait()
 
 
 def solution(mesh):

time: 45.9 us -> 44.4 us (0.967)
  local copies, waits for them, and re-layouts: 1.44 us -> 0 us
    unnamed x2 -> x0, local copies, waits for them, and re-layouts: 1.44 us -> none
    pallas_call x1, Pallas kernels: 43.7 us -> 42.8 us  [on_device(): pl.pallas_call(functools.partial(kernel, sizes), out_shape=(pltpu.VMEM((X...]
    pallas_call x0 -> x1, Pallas kernels: none -> 0.85 us  [on_device(): pl.pallas_call(write_out, out_shape=tuple((jax.ShapeDtypeStruct(v.shape,...]
where the time goes in v7:
time: 44.4 us; the launch traced here: 44.3 us
  Pallas kernels  43.7 us (98%)
  between operations  0.64 us (1%)
    pallas_call x1, Pallas kernels, on_device(): pl.pallas_call(functools.partial(kernel, sizes), out_shape=(pltpu.VMEM((X...  42.8 us

profile of v7, /device:TPU:0, one launch (start us, length us, event | category | flops | bytes accessed | tf_op | source)
XLA Modules:
  0.0 44.3 jit_solution(3015792878616693850)
XLA Ops:
  0.6 42.8 %shard_map.50 = (f32[4,16,128]{2,1,0:T(8,128)S(1)}, f32[19,4,16,128]{3,2,1,0:T(8,128)S(1)}) custom-call(f32[4,16,128]{2,1,0:T(8,128)} %order_in.1, f32[4,16,128]{2,1,0:T(8,128)} %dens_in.1, f32[3,4,16,128]{3,2,1,0:T(8,128)} %vel_in.1), custom_call_target="tpu_custom_call" | custom-call | tf_op jit(solution)/shard_map/pallas_call | solution.py:696
  43.5 0.8 %shard_map.51 = (f32[4,16,128]{2,1,0:T(8,128)}, f32[19,4,16,128]{3,2,1,0:T(8,128)}) custom-call(f32[4,16,128]{2,1,0:T(8,128)S(1)} %get-tuple-element.4.order, f32[19,4,16,128]{3,2,1,0:T(8,128)S(1)} %get-tuple-element.5.pops), custom_call_target="tpu_custom_call" | custom-call | tf_op jit(solution)/shard_map/pallas_call | solution.py:706

commit v8 on v7

--- a/solution.py
+++ b/solution.py
@@ -64,6 +64,8 @@
     block = 2 * DEEP
     width = X * block
     me = [lax.axis_index(a) for a in AXES]
+    tiles = Y // 8
+    singles = (MOMS + 6 + DEEP) * tiles
     zsides = (1,) if sizes[2] == 2 else SIGNS
 
     def device(off):
@@ -195,7 +197,7 @@
             dst = fz.at[par, INDEX[c], TRAVEL[a]]
             rows = {1: pl.ds(Y - DEEP, DEEP), -1: pl.ds(0, DEEP), 0: pl.ds(0, Y)}[b]
             land = pl.ds({1: E - DEEP, -1: Y, 0: 0}[b], DEEP if b else Y)
-            planes = pl.ds(0, 1 if a and b else 2)
+            planes = pl.ds(0, 1 if a else 2)
             messages.append((sz.at[planes, rows, :], dst.at[planes, land, :], (a, b, c)))
 
         for c in zsides:
@@ -309,6 +311,11 @@
                 first = place(first, v, g, x)
             for k, (up, down) in enumerate(ZPAIRS):
                 second = place(second, jnp.where(low_col, out[down], out[up]), k, x)
+        for a in SIGNS:
+            up, down = ZPAIRS[TRAVEL[a]]
+            v = jnp.where(low_col, pops[down, xsrc(a)], pops[up, xsrc(a)])
+            at = 5 * width + 2 * INDEX[a]
+            first = jnp.where((lane >= at) & (lane < at + 2), roll(v, at + 1, 1), first)
         sz[0] = first
         sz[1] = second
         for s in SIGNS:
@@ -321,16 +328,20 @@
     def ready_planes():
         for s in SIGNS:
             si, edge = INDEX[s], xsrc(s)
+
+            def keep_plane(k, v):
+                sx[si, k * tiles : (k + 1) * tiles] = v.reshape(tiles, 8, Z)
+
             for g in range(MOMS):
-                sx[si, g] = mom[g, edge]
+                keep_plane(g, mom[g, edge])
             for k, i in enumerate(CROSS[0][s]):
-                sx[si, MOMS + k] = pops[i, edge]
+                keep_plane(MOMS + k, pops[i, edge])
             for slot in range(DEEP):
                 x = slot + (X - DEEP if s == 1 else 0)
-                sx[si, MOMS + 5 + slot] = base[x]
-                sx[si, MOMS + 6 + DEEP, slot : slot + 1, :] = mom[2, x, 0:1, :]
-                sx[si, MOMS + 6 + DEEP, DEEP + slot : DEEP + slot + 1, :] = mom[2, x, Y - 1 :, :]
-            sx[si, MOMS + 5 + DEEP] = sz[0]
+                keep_plane(MOMS + 5 + slot, base[x])
+                sx[si, singles, slot : slot + 1, :] = mom[2, x, 0:1, :]
+                sx[si, singles, DEEP + slot : DEEP + slot + 1, :] = mom[2, x, Y - 1 :, :]
+            keep_plane(MOMS + 5 + DEEP, sz[0])
 
     def send(par):
         messages, ssem, rsem = bundle(par)
@@ -389,21 +400,20 @@
         finish(*bundle(par))
         low, high = ry.at[par, 0], ry.at[par, 1]
 
+        def came(si, k):
+            return rx[par, si, k * tiles : (k + 1) * tiles].reshape(Y, Z)
+
         def tall(a):
             if a == 0:
                 near = extend(sz[0], low[1], high[1])
             else:
-                mid, at = rx[par, INDEX[a], MOMS + 5 + DEEP], DEEP + 1
+                mid, at = came(INDEX[a], MOMS + 5 + DEEP), DEEP + 1
                 near = extend(mid, rxy[par, 0, INDEX[a], at], rxy[par, 1, INDEX[a], at])
             far = [fz[par, INDEX[c], TRAVEL[a], 0] for c in zsides]
             halves = [jnp.where(facing, far[0], near), jnp.where(facing, near, far[-1])]
             return [roll(v, -a * width, 1) for v in halves]
 
         parts = [tall(a) for a in (0, 1, -1)]
-        ends = [
-            [roll(fz[par, INDEX[c], TRAVEL[a], 1], -a * width, 1) for a in (0, 1, -1)] for c in zsides
-        ]
-
         def gather(three, slot, add):
             at = slot * width
             rel = lax.rem(elane + (Z - at), Z)
@@ -415,10 +425,19 @@
             return jnp.where(left, halves[0], halves[1])
 
         def packed_far(slot):
-            halves = [gather(three, slot, HALF * k) for k, three in enumerate(ends)]
-            if len(halves) == 1:
-                halves.append(roll(halves[0], HALF, 1))
-            return jnp.where(left, halves[0], halves[1])
+            shift, halves = (DEEP - slot * X) * block, []
+            for k, c in enumerate(SIGNS):
+                far = fz[par, INDEX[c if c in zsides else 1], TRAVEL[0], 1]
+                halves.append(roll(far, shift + HALF * k, 1))
+            v = jnp.where(left, halves[0], halves[1])
+            for a in SIGNS:
+                if slot == TRAVEL[a]:
+                    at = 5 * width + 2 * INDEX[a]
+                    to = ((-1 if a == 1 else X) + DEEP) * block + DEEP - 1
+                    for c, far, add in ((1, 0, 0), (-1, 1, HALF + 1)):
+                        one = fz[par, INDEX[c if c in zsides else 1], TRAVEL[a], 0]
+                        v = jnp.where(elane == to + add, roll(one, to + add - at - far, 1), v)
+            return v
 
         rho_z = packed(1)
         u_z = [packed(2 + d) for d in range(3)]
@@ -439,9 +458,9 @@
 
         def speed(px):
             if px < 0:
-                tiles, mid = [rxy[par, k, 0, DEEP] for k in range(2)], rx[par, 0, 1]
+                tiles, mid = [rxy[par, k, 0, DEEP] for k in range(2)], came(0, 1)
             elif px >= X:
-                tiles, mid = [rxy[par, k, 1, DEEP] for k in range(2)], rx[par, 1, 1]
+                tiles, mid = [rxy[par, k, 1, DEEP] for k in range(2)], came(1, 1)
             else:
                 tiles, mid = [ry[par, k, 0 if px == 0 else X + 2] for k in range(2)], mom[1, px]
             return extend(mid, tiles[0], tiles[1])
@@ -464,7 +483,7 @@
                 return mom[2, px, y : y + 1, :]
             side, slot = (0, px + DEEP) if px < 0 else (1, px - X)
             at = slot if s == 1 else DEEP + slot
-            return rx[par, side, MOMS + 6 + DEEP, at : at + 1, :]
+            return rx[par, side, singles, at : at + 1, :]
 
         across = {}
         for lo, hi in ((-1, 0), (X - 1, X)):
@@ -499,9 +518,9 @@
 
         def complete(px):
             if px < 0:
-                mid = rx[par, 0, MOMS + 5 + px + DEEP]
+                mid = came(0, MOMS + 5 + px + DEEP)
             elif px >= X:
-                mid = rx[par, 1, MOMS + 5 + px - X]
+                mid = came(1, MOMS + 5 + px - X)
             else:
                 mid = base[px]
             v = extend(mid, around(px, 1), around(px, -1))
@@ -562,11 +581,11 @@
                 return
             a = 1 if px < 0 else -1
             ai = INDEX[a]
-            rho = rx[par, ai, 0]
-            u = [rx[par, ai, 1 + d] for d in range(3)]
+            rho = came(ai, 0)
+            u = [came(ai, 1 + d) for d in range(3)]
             hit = collide(rho, u, [f[own_rows, :] for f in F[px]])
             for k, i in enumerate(CROSS[0][a]):
-                XH[i] = hit(i, rx[par, ai, MOMS + k], along)
+                XH[i] = hit(i, came(ai, MOMS + k), along)
             for s in SIGNS:
                 i = DIRS.index((a, s, 0))
                 r = deep_row(0, s)
@@ -678,13 +697,13 @@
     X, Y, Z = order_param.shape
     f32 = jnp.float32
     plane, rows, tall = (Y, Z), (8, Z), (Y + 8, Z)
-    planes = MOMS + 5 + DEEP + 2
-    lines = 2 * planes * Y + 2 * 8 * (MOMS + 4) + 4 * (DEEP + 3) * DEEP
-    lines += (1 if sizes[2] == 2 else 2) * (6 * Y + 8 * DEEP)
+    stack = (MOMS + 5 + DEEP + 1) * (Y // 8) + 1
+    lines = 2 * 8 * stack + 2 * 8 * (MOMS + 4) + 4 * (DEEP + 3) * DEEP
+    lines += (1 if sizes[2] == 2 else 2) * (4 * Y + 8 * DEEP)
     vmem = [
         (19, X, Y, Z), (MOMS, X, Y, Z), (X, Y, Z), (X + 2 * DEEP,) + tall, tall,
         (X, Y, Z), (3, X, Y, Z), (lines, Z),
-        (2, planes) + plane, (2, 2, planes) + plane,
+        (2, stack) + rows, (2, 2, stack) + rows,
         (2, MOMS + 4) + rows, (2, 2, MOMS + 4) + rows,
         (2, 2, DEEP + 3) + rows, (2, 2, 2, DEEP + 3) + rows,
         (2,) + plane, (2, 2, 3, 2) + tall, (2, 3) + rows, (2,) + rows,

time: 44.4 us -> 43.6 us (0.982)
  Pallas kernels: 43.7 us -> 42.8 us
    pallas_call x1, Pallas kernels: 42.8 us -> 42 us  [on_device(): pl.pallas_call(functools.partial(kernel, sizes), out_shape=(pltpu.VMEM((X...]
where the time goes in v8:
time: 43.6 us; the launch traced here: 43.4 us
  Pallas kernels  42.8 us (98%)
  between operations  0.64 us (1%)
    pallas_call x1, Pallas kernels, on_device(): pl.pallas_call(functools.partial(kernel, sizes), out_shape=(pltpu.VMEM((X...  42 us

profile of v8, /device:TPU:0, one launch (start us, length us, event | category | flops | bytes accessed | tf_op | source)
XLA Modules:
  0.0 43.4 jit_solution(17796465061791525055)
XLA Ops:
  0.6 42.0 %shard_map.50 = (f32[4,16,128]{2,1,0:T(8,128)S(1)}, f32[19,4,16,128]{3,2,1,0:T(8,128)S(1)}) custom-call(f32[4,16,128]{2,1,0:T(8,128)} %order_in.1, f32[4,16,128]{2,1,0:T(8,128)} %dens_in.1, f32[3,4,16,128]{3,2,1,0:T(8,128)} %vel_in.1), custom_call_target="tpu_custom_call" | custom-call | tf_op jit(solution)/shard_map/pallas_call | solution.py:715
  42.6 0.8 %shard_map.51 = (f32[4,16,128]{2,1,0:T(8,128)}, f32[19,4,16,128]{3,2,1,0:T(8,128)}) custom-call(f32[4,16,128]{2,1,0:T(8,128)S(1)} %get-tuple-element.4.order, f32[19,4,16,128]{3,2,1,0:T(8,128)S(1)} %get-tuple-element.5.pops), custom_call_target="tpu_custom_call" | custom-call | tf_op jit(solution)/shard_map/pallas_call | solution.py:725

commit v9 on v8

--- a/solution.py
+++ b/solution.py
@@ -640,6 +640,18 @@
             for d in range(3):
                 mom[1 + d, x] = flows[x][d]
 
+        tx = {0: 0.0, X: 0.0}
+        for x in range(1, X):
+            tx[x] = (flows[x][0] + flows[x - 1][0]) * (O[x] + O[x - 1])
+        for x in range(X):
+            f, o = flows[x], O[x]
+            ty = jnp.where(row == 0, 0.0, (f[1] + roll(f[1], 1, 0)) * (o + roll(o, 1, 0)))
+            tz = jnp.where(lane == 0, 0.0, (f[2] + roll(f[2], 1, 1)) * (o + roll(o, 1, 1)))
+            change = tx[x + 1] - tx[x] + (roll(ty, -1, 0) - ty) + (roll(tz, -1, 1) - tz)
+            base[x] = base[x] - 0.25 * change
+
+        ready()
+
         @pl.when(n == ITERS - 1)
         def _():
             for s in SIGNS:
@@ -650,19 +662,8 @@
                 cz_[INDEX[s]] = pack([mom[3, x] for x in range(X)], s)
             launch(*farewell())
 
-        tx = {0: 0.0, X: 0.0}
-        for x in range(1, X):
-            tx[x] = (flows[x][0] + flows[x - 1][0]) * (O[x] + O[x - 1])
-        for x in range(X):
-            f, o = flows[x], O[x]
-            ty = jnp.where(row == 0, 0.0, (f[1] + roll(f[1], 1, 0)) * (o + roll(o, 1, 0)))
-            tz = jnp.where(lane == 0, 0.0, (f[2] + roll(f[2], 1, 1)) * (o + roll(o, 1, 1)))
-            change = tx[x + 1] - tx[x] + (roll(ty, -1, 0) - ty) + (roll(tz, -1, 1) - tz)
-            base[x] = base[x] - 0.25 * change
-
         @pl.when(n < ITERS - 1)
         def _():
-            ready()
             send(1 - par)
 
         return carry

time: 43.6 us -> 43.4 us (level)
  no operation moved by 1% of the time
where the time goes in v9:
time: 43.4 us; the launch traced here: 43.3 us
  Pallas kernels  42.6 us (98%)
  between operations  0.64 us (1%)
    pallas_call x1, Pallas kernels, on_device(): pl.pallas_call(functools.partial(kernel, sizes), out_shape=(pltpu.VMEM((X...  41.8 us

profile of v9, /device:TPU:0, one launch (start us, length us, event | category | flops | bytes accessed | tf_op | source)
XLA Modules:
  0.0 43.3 jit_solution(5042699318325820323)
XLA Ops:
  0.6 41.8 %shard_map.50 = (f32[4,16,128]{2,1,0:T(8,128)S(1)}, f32[19,4,16,128]{3,2,1,0:T(8,128)S(1)}) custom-call(f32[4,16,128]{2,1,0:T(8,128)} %order_in.1, f32[4,16,128]{2,1,0:T(8,128)} %dens_in.1, f32[3,4,16,128]{3,2,1,0:T(8,128)} %vel_in.1), custom_call_target="tpu_custom_call" | custom-call | tf_op jit(solution)/shard_map/pallas_call | solution.py:716
  42.4 0.8 %shard_map.51 = (f32[4,16,128]{2,1,0:T(8,128)}, f32[19,4,16,128]{3,2,1,0:T(8,128)}) custom-call(f32[4,16,128]{2,1,0:T(8,128)S(1)} %get-tuple-element.4.order, f32[19,4,16,128]{3,2,1,0:T(8,128)S(1)} %get-tuple-element.5.pops), custom_call_target="tpu_custom_call" | custom-call | tf_op jit(solution)/shard_map/pallas_call | solution.py:726
